TPU v7x, 32 devices: a whole 2x2x4 slice. The times are simulated.
32 devices in a mesh: exp: 8 (over z, y), tp: 4 (over x, core).
Axes of the slice: x: 2, y: 2, z: 4, core: 2. Of those that a mesh axis runs over, the one named last changes fastest.
Arguments:
- tokens: bfloat16 [2048, 2048], P('exp'), may hold values from -6 to 6
- cotangent: bfloat16 [2048, 2048], P('exp'), may hold values from -12 to 12
- seq_start: int32 [2048], P('exp'), may hold values from 0 to 248, as said below
- routes: int32 [2048, 8], P('exp'), may hold values from 0 to 31, all different within a row; in each aligned block of 256 rows (0 to 255, 256 to 511, ...) at most 96 rows name the same one
- norm1_gain: float32 [2048], replicated, may hold values from 0.25 to 1.75
- norm2_gain: float32 [2048], replicated, may hold values from 0.25 to 1.75
- q_gain: float32 [128], replicated, may hold values from 0.25 to 1.75
- k_gain: float32 [128], replicated, may hold values from 0.25 to 1.75
- query_matrix: bfloat16 [2048, 4096], P(None, 'tp'), may hold values from -0.125 to 0.125
- key_matrix: bfloat16 [2048, 512], P(None, 'tp'), may hold values from -0.125 to 0.125
- value_matrix: bfloat16 [2048, 512], P(None, 'tp'), may hold values from -0.125 to 0.125
- output_matrix: bfloat16 [2048, 4096], P(None, 'tp'), may hold values from -0.75 to 0.75
- w_router: bfloat16 [2048, 32], replicated, may hold values from -0.125 to 0.125
- w_gate: bfloat16 [32, 2048, 768], P('exp', None, 'tp'), may hold values from -0.125 to 0.125
- w_up: bfloat16 [32, 2048, 768], P('exp', None, 'tp'), may hold values from -0.125 to 0.125
- w_down: bfloat16 [32, 768, 2048], P('exp', 'tp'), may hold values from -0.4375 to 0.4375
Outputs:
- layer_out: bfloat16 [2048, 2048], P('exp')
- grad_tokens: bfloat16 [2048, 2048], P('exp')
- grad_norm1: float32 [2048], replicated
- grad_norm2: float32 [2048], replicated
- grad_q_gain: float32 [128], replicated
- grad_k_gain: float32 [128], replicated
- grad_query: float32 [2048, 4096], P('exp', 'tp')
- grad_key: float32 [2048, 512], P('exp', 'tp')
- grad_value: float32 [2048, 512], P('exp', 'tp')
- grad_out: float32 [2048, 4096], P('exp', 'tp')
- grad_router: float32 [2048, 32], P('exp')
- grad_gate: float32 [32, 2048, 768], P('exp', None, 'tp')
- grad_up: float32 [32, 2048, 768], P('exp', None, 'tp')
- grad_down: float32 [32, 768, 2048], P('exp', 'tp')
Inputs may be any that keep to these rules, and one draw needn't show every extreme that they name: Sequences never cross a block of 256 rows; each block begins with a sequence of exactly 128 rows and no sequence is longer; seq_start never falls within a block and is at most the row's own index there; each block's last sequence begins at row 248. `routes`: each token names 8 different experts; among the 256 rows of one index of exp no expert is named by more than 96 rows, a bound that some block reaches.
All inputs are finite; a program needn't handle non-finite values.
Results may differ from a plain program's by a relative error of at most 0.022.
Values may be sent and summed in bfloat16 or wider, within the bound.
A program may use at most 320 MiB of HBM per device.

v0:
```python
import jax
import jax.numpy as jnp
from jax import lax
from jax.sharding import PartitionSpec as P

HEAD_DIMENSION = 128
TOPK = 8


EPSILON = 1e-06
ROPE_BASE = 1000000.0
MASKED = -1e30


def rotate_normed(pre_proj, gain_vec, positions):
    normed = (
        pre_proj * lax.rsqrt(jnp.mean(pre_proj * pre_proj, -1, keepdims=True) + EPSILON) * gain_vec
    )
    half_dim = HEAD_DIMENSION // 2
    freqs = ROPE_BASE ** (-(jnp.arange(half_dim).astype(jnp.float32) * 2.0 / HEAD_DIMENSION))
    angles = positions.reshape((-1,) + (1,) * (normed.ndim - 2) + (1,)) * freqs
    cosine = jnp.cos(angles)
    sine = jnp.sin(angles)
    first_half = normed[..., :half_dim]
    second_half = normed[..., half_dim:]
    return jnp.concatenate(
        [first_half * cosine - second_half * sine, second_half * cosine + first_half * sine], -1
    )


def masked_scores(query_blk, key_rot, query_rows, query_start, key_start):
    scores = jnp.einsum(
        "igrd,jgd->grij", query_blk, key_rot, preferred_element_type=jnp.float32
    ) * HEAD_DIMENSION ** (-0.5)
    key_rows = jnp.arange(key_rot.shape[0])
    allowed = (key_rows[None, :] <= query_rows[:, None]) & (
        key_start[None, :] == query_start[:, None]
    )
    return jnp.where(allowed[None, None], scores, MASKED)


def attend_forward(query_rot, key_rot, value_half_precision, query_rows, query_start, key_start):
    scores = masked_scores(query_rot, key_rot, query_rows, query_start, key_start)
    peak = jnp.max(scores, -1, keepdims=True)
    weights = jnp.exp(scores - peak)
    totals = jnp.sum(weights, -1, keepdims=True)
    log_total = (peak + jnp.log(totals))[..., 0]
    probs = (weights / totals).astype(jnp.bfloat16)
    attended = jnp.einsum(
        "grij,jgd->igrd", probs, value_half_precision, preferred_element_type=jnp.float32
    )
    return (attended.astype(jnp.bfloat16), log_total)


def attend_backward(
    query_rot,
    key_rot,
    value_half_precision,
    attended_bf,
    log_total,
    grad_att,
    query_rows,
    query_start,
    key_start,
):
    scores = masked_scores(query_rot, key_rot, query_rows, query_start, key_start)
    probs = jnp.exp(scores - log_total[..., None])
    probs_bf = probs.astype(jnp.bfloat16)
    grad_value = jnp.einsum(
        "grij,igrd->jgd", probs_bf, grad_att, preferred_element_type=jnp.float32
    )
    grad_probs = jnp.einsum(
        "igrd,jgd->grij", grad_att, value_half_precision, preferred_element_type=jnp.float32
    )
    delta = jnp.sum(grad_att.astype(jnp.float32) * attended_bf.astype(jnp.float32), -1)
    grad_scores = (probs * (grad_probs - jnp.transpose(delta, (1, 2, 0))[..., None])).astype(
        jnp.bfloat16
    )
    scale = HEAD_DIMENSION ** (-0.5)
    grad_query = (
        jnp.einsum("grij,jgd->igrd", grad_scores, key_rot, preferred_element_type=jnp.float32)
        * scale
    )
    grad_key = (
        jnp.einsum("grij,igrd->jgd", grad_scores, query_rot, preferred_element_type=jnp.float32)
        * scale
    )
    return (grad_query, grad_key, grad_value)


def to_owner(buffer_rows):
    arrived = lax.all_to_all(buffer_rows, "exp", split_axis=0, concat_axis=0, tiled=True)
    return arrived


def body(
    tokens,
    cotangent,
    seq_start,
    routes,
    norm1_gain,
    norm2_gain,
    q_gain,
    k_gain,
    query_matrix,
    key_matrix,
    value_matrix,
    output_matrix,
    w_router,
    w_gate,
    w_up,
    w_down,
):
    tok_rows, model_width = tokens.shape
    kv_groups = key_matrix.shape[1] // HEAD_DIMENSION
    q_heads = query_matrix.shape[1] // HEAD_DIMENSION
    group_repeats = q_heads // kv_groups
    all_experts = w_router.shape[1]
    local_experts = w_gate.shape[0]
    owners = all_experts // local_experts
    capacity = 3 * tok_rows * TOPK // (2 * all_experts)
    contract_last = (((1,), (1,)), ((), ()))
    contract_first = (((0,), (0,)), ((), ()))
    resid = tokens.astype(jnp.float32)
    scale_one = lax.rsqrt(jnp.mean(resid * resid, -1, keepdims=True) + EPSILON)
    first_normalized = (resid * scale_one * norm1_gain).astype(jnp.bfloat16)
    positions = (jnp.arange(tok_rows) - seq_start).astype(jnp.float32)
    query_before_norm = jnp.dot(
        first_normalized, query_matrix, preferred_element_type=jnp.float32
    ).reshape(tok_rows, kv_groups, group_repeats, HEAD_DIMENSION)
    key_before_norm = jnp.dot(
        first_normalized, key_matrix, preferred_element_type=jnp.float32
    ).reshape(tok_rows, kv_groups, HEAD_DIMENSION)
    value_half_precision = (
        jnp.dot(first_normalized, value_matrix, preferred_element_type=jnp.float32)
        .astype(jnp.bfloat16)
        .reshape(tok_rows, kv_groups, HEAD_DIMENSION)
    )
    q_rot, q_back = jax.vjp(
        lambda pre_vals, gain_vals: rotate_normed(pre_vals, gain_vals, positions),
        query_before_norm,
        q_gain,
    )
    k_rot, k_back = jax.vjp(
        lambda pre_vals, gain_vals: rotate_normed(pre_vals, gain_vals, positions),
        key_before_norm,
        k_gain,
    )
    q_rot_bf = q_rot.astype(jnp.bfloat16)
    k_rot_bf = k_rot.astype(jnp.bfloat16)
    row_ids = jnp.arange(tok_rows)
    attended_blk, lse_blk = attend_forward(
        q_rot_bf, k_rot_bf, value_half_precision, row_ids, seq_start, seq_start
    )
    attended_flat = attended_blk.reshape(tok_rows, q_heads * HEAD_DIMENSION)
    attn_part = lax.dot_general(
        attended_flat, output_matrix, contract_last, preferred_element_type=jnp.float32
    )
    after_attn = resid + lax.psum(attn_part, "tp")
    scale_two = lax.rsqrt(jnp.mean(after_attn * after_attn, -1, keepdims=True) + EPSILON)
    normed_two = (after_attn * scale_two * norm2_gain).astype(jnp.bfloat16)
    logits = jnp.dot(normed_two, w_router, preferred_element_type=jnp.float32)
    chosen = jnp.take_along_axis(logits, routes, 1)
    gates = jax.nn.softmax(chosen, -1)
    flat_routes = routes.reshape(-1)
    one_hot = (flat_routes[:, None] == jnp.arange(all_experts)[None, :]).astype(jnp.int32)
    slots = jnp.sum(jnp.cumsum(one_hot, 0) * one_hot, 1) - 1
    places = flat_routes * capacity + slots
    send_fwd = (
        jnp.zeros((all_experts * capacity, model_width), jnp.bfloat16)
        .at[places]
        .set(jnp.repeat(normed_two, TOPK, 0))
    )
    received = to_owner(send_fwd.reshape(owners, local_experts, capacity, model_width))
    gate_pre = jnp.einsum("sjcd,jdf->sjcf", received, w_gate, preferred_element_type=jnp.float32)
    up_pre = jnp.einsum("sjcd,jdf->sjcf", received, w_up, preferred_element_type=jnp.float32)
    sigmoid_g = jax.nn.sigmoid(gate_pre)
    silu_g = gate_pre * sigmoid_g
    hidden = (silu_g * up_pre).astype(jnp.bfloat16)
    expert_part = jnp.einsum(
        "sjcf,jfd->sjcd", hidden, w_down, preferred_element_type=jnp.float32
    ).astype(jnp.bfloat16)
    grad_y = cotangent.astype(jnp.float32)
    came_back = lax.all_to_all(expert_part, "exp", split_axis=0, concat_axis=0, tiled=True).reshape(
        all_experts * capacity, model_width
    )
    picked = came_back[places].astype(jnp.float32).reshape(tok_rows, TOPK, model_width)
    mixture = lax.psum(jnp.sum(gates[..., None] * picked, 1).astype(jnp.bfloat16), "tp").astype(
        jnp.float32
    )
    gates_part = jnp.sum(grad_y[:, None, :] * picked, -1)
    layer_out = (after_attn + mixture).astype(jnp.bfloat16)
    expert_grad = (
        (gates[..., None] * grad_y[:, None, :])
        .astype(jnp.bfloat16)
        .reshape(tok_rows * TOPK, model_width)
    )
    send_back = (
        jnp.zeros((all_experts * capacity, model_width), jnp.bfloat16).at[places].set(expert_grad)
    )
    received_grad = to_owner(send_back.reshape(owners, local_experts, capacity, model_width))
    grad_hidden = jnp.einsum(
        "sjcd,jfd->sjcf", received_grad, w_down, preferred_element_type=jnp.float32
    )
    grad_gate_pre = (
        grad_hidden * up_pre * sigmoid_g * (1.0 + gate_pre * (1.0 - sigmoid_g))
    ).astype(jnp.bfloat16)
    grad_up_pre = (grad_hidden * silu_g).astype(jnp.bfloat16)
    grad_down = jnp.einsum(
        "sjcf,sjcd->jfd", hidden, received_grad, preferred_element_type=jnp.float32
    )
    grad_gate = jnp.einsum(
        "sjcd,sjcf->jdf", received, grad_gate_pre, preferred_element_type=jnp.float32
    )
    grad_up = jnp.einsum(
        "sjcd,sjcf->jdf", received, grad_up_pre, preferred_element_type=jnp.float32
    )
    expert_input_grad = jnp.einsum(
        "sjcf,jdf->sjcd", grad_gate_pre, w_gate, preferred_element_type=jnp.float32
    )
    expert_input_grad = (
        expert_input_grad
        + jnp.einsum("sjcf,jdf->sjcd", grad_up_pre, w_up, preferred_element_type=jnp.float32)
    ).astype(jnp.bfloat16)
    grads_back = lax.all_to_all(
        expert_input_grad, "exp", split_axis=0, concat_axis=0, tiled=True
    ).reshape(all_experts * capacity, model_width)
    moe_input_part = jnp.sum(
        grads_back[places].astype(jnp.float32).reshape(tok_rows, TOPK, model_width), 1
    )
    moe_input_grad, grad_gates = (
        lax.psum(moe_input_part.astype(jnp.bfloat16), "tp").astype(jnp.float32),
        lax.psum(gates_part.astype(jnp.bfloat16), "tp").astype(jnp.float32),
    )
    grad_chosen = gates * (grad_gates - jnp.sum(gates * grad_gates, -1, keepdims=True))
    grad_logits = jnp.sum(
        (routes[:, :, None] == jnp.arange(all_experts)[None, None, :]).astype(jnp.float32)
        * grad_chosen[..., None],
        1,
    ).astype(jnp.bfloat16)
    router_part = lax.dot_general(
        normed_two, grad_logits, contract_first, preferred_element_type=jnp.float32
    )
    grad_normed_two = moe_input_grad + lax.dot_general(
        grad_logits, w_router, contract_last, preferred_element_type=jnp.float32
    )
    gain2_scaled = grad_normed_two * norm2_gain
    norm2_part = jnp.sum(grad_normed_two * after_attn * scale_two, 0)
    grad_resid = (
        grad_y
        + scale_two * gain2_scaled
        - after_attn * scale_two**3 * jnp.mean(gain2_scaled * after_attn, -1, keepdims=True)
    )
    residual_gradient_half = grad_resid.astype(jnp.bfloat16)
    out_part = lax.dot_general(
        residual_gradient_half, attended_flat, contract_first, preferred_element_type=jnp.float32
    )
    attended_gradient = (
        jnp.dot(residual_gradient_half, output_matrix, preferred_element_type=jnp.float32)
        .astype(jnp.bfloat16)
        .reshape(tok_rows, kv_groups, group_repeats, HEAD_DIMENSION)
    )
    grad_q_blk, grad_k_blk, grad_v_blk = attend_backward(
        q_rot_bf,
        k_rot_bf,
        value_half_precision,
        attended_blk,
        lse_blk,
        attended_gradient,
        row_ids,
        seq_start,
        seq_start,
    )
    grad_q_pre, q_gain_part = q_back(grad_q_blk)
    grad_k_pre, k_gain_part = k_back(grad_k_blk)
    grad_query_bf = grad_q_pre.reshape(tok_rows, q_heads * HEAD_DIMENSION).astype(jnp.bfloat16)
    key_gradient_half = grad_k_pre.reshape(tok_rows, kv_groups * HEAD_DIMENSION).astype(
        jnp.bfloat16
    )
    value_gradient_half = grad_v_blk.reshape(tok_rows, kv_groups * HEAD_DIMENSION).astype(
        jnp.bfloat16
    )
    query_part = lax.dot_general(
        first_normalized, grad_query_bf, contract_first, preferred_element_type=jnp.float32
    )
    key_part = lax.dot_general(
        first_normalized, key_gradient_half, contract_first, preferred_element_type=jnp.float32
    )
    value_part = lax.dot_general(
        first_normalized, value_gradient_half, contract_first, preferred_element_type=jnp.float32
    )
    input_part = lax.dot_general(
        grad_query_bf, query_matrix, contract_last, preferred_element_type=jnp.float32
    )
    input_part = input_part + lax.dot_general(
        key_gradient_half, key_matrix, contract_last, preferred_element_type=jnp.float32
    )
    input_part = input_part + lax.dot_general(
        value_gradient_half, value_matrix, contract_last, preferred_element_type=jnp.float32
    )
    grad_normed_one, q_gain_group, k_gain_group = (
        lax.psum(input_part.astype(jnp.bfloat16), "tp").astype(jnp.float32),
        lax.psum(q_gain_part.astype(jnp.bfloat16), "tp").astype(jnp.float32),
        lax.psum(k_gain_part.astype(jnp.bfloat16), "tp").astype(jnp.float32),
    )
    gain1_scaled = grad_normed_one * norm1_gain
    norm1_part = jnp.sum(grad_normed_one * resid * scale_one, 0)
    grad_tokens = (
        grad_resid
        + scale_one * gain1_scaled
        - resid * scale_one**3 * jnp.mean(gain1_scaled * resid, -1, keepdims=True)
    ).astype(jnp.bfloat16)
    grad_query, grad_key, grad_value, grad_out, grad_router = (
        lax.psum_scatter(
            query_part.astype(jnp.bfloat16), "exp", scatter_dimension=0, tiled=True
        ).astype(jnp.float32),
        lax.psum_scatter(
            key_part.astype(jnp.bfloat16), "exp", scatter_dimension=0, tiled=True
        ).astype(jnp.float32),
        lax.psum_scatter(
            value_part.astype(jnp.bfloat16), "exp", scatter_dimension=0, tiled=True
        ).astype(jnp.float32),
        lax.psum_scatter(
            out_part.astype(jnp.bfloat16), "exp", scatter_dimension=0, tiled=True
        ).astype(jnp.float32),
        lax.psum_scatter(
            router_part.astype(jnp.bfloat16), "exp", scatter_dimension=0, tiled=True
        ).astype(jnp.float32),
    )
    grad_norm1, grad_norm2, grad_q_gain, grad_k_gain = lax.psum(
        (norm1_part, norm2_part, q_gain_group, k_gain_group), "exp"
    )
    return (
        layer_out,
        grad_tokens,
        grad_norm1,
        grad_norm2,
        grad_q_gain,
        grad_k_gain,
        grad_query,
        grad_key,
        grad_value,
        grad_out,
        grad_router,
        grad_gate,
        grad_up,
        grad_down,
    )


def solution(mesh):
    placed = (
        P("exp", None),
        P("exp", None),
        P("exp"),
        P("exp", None),
        P(),
        P(),
        P(),
        P(),
        P(None, "tp"),
        P(None, "tp"),
        P(None, "tp"),
        P(None, "tp"),
        P(),
        P("exp", None, "tp"),
        P("exp", None, "tp"),
        P("exp", "tp", None),
    )
    return jax.shard_map(
        body,
        mesh=mesh,
        in_specs=placed,
        out_specs=(
            P("exp", None),
            P("exp", None),
            P(),
            P(),
            P(),
            P(),
            P("exp", "tp"),
            P("exp", "tp"),
            P("exp", "tp"),
            P("exp", "tp"),
            P("exp", None),
            P("exp", None, "tp"),
            P("exp", None, "tp"),
            P("exp", "tp", None),
        ),
        check_vma=False,
    )
```

profile of v0, /device:TPU:0, one launch (start us, length us, event | category | flops | bytes accessed | tf_op | source)
XLA Modules:
  0.0 1758.3 jit_solution(9744592429919413193)
XLA Ops:
  11.8 2.6 fusion.63
  26.0 2.6 fusion.118
  30.6 16.4 reduce-window.6
  49.5 33.3 %all-reduce.11.cloned.1.call-done = f32[256,2048]{1,0:T(8,128)} async-done(((f32[256,2048]{1,0:T(8,128)}), f32[256,2048]{1,0:T(8,128)}) %all-reduce.11.cloned.1.call-update) | async-done | bytes 2097168 | tf_op jit(solution)/shard_map/psum | solution.py:159
  82.9 2.2 multiply_reduce_fusion.2
  87.7 19.6 %scatter_custom_fusion = bf16[3072,2048]{1,0:T(8,128)(2,1)} fusion(s32[2048]{0:T(1024)S(1)} %bitcast.273, bf16[]{:T(256)} %constant.68.clone.1, bf16[256,2048]{1,0:T(8,128)(2,1)} %multiply_convert_fusion), kind=kCustom, calls=%fused_computation.24 | custom fusion | bytes 13631490 | tf_op jit(solution)/shard_map/scatter | solution.py:172
  107.2 5.7 all-to-all-start
  113.2 2.9 convert_element_type.243
  116.5 16.8 gather_fusion.2
  133.8 20.2 %scatter_custom_fusion.1 = bf16[3072,2048]{1,0:T(8,128)(2,1)} fusion(s32[2048]{0:T(1024)S(1)} %bitcast.274, f32[256,2048]{1,0:T(8,128)} %convert_element_type.243, f32[2048]{0:T(1024)S(1)} %mul.588, bf16[]{:T(256)} %constant.68.clone.1), kind=kCustom, calls=%fused_computation.22 | custom fusion | flops 8388608 | bytes 14688258 | tf_op jit(solution)/shard_map/scatter | solution.py:199
  154.1 231.7 %all-to-all-done = bf16[8,4,96,2048]{3,2,1,0:T(8,128)(2,1)} async-done(((bf16[8,4,96,2048]{3,2,1,0:T(8,128)(2,1)}), bf16[8,4,96,2048]{3,2,1,0:T(8,128)(2,1)}, u32[]{:S(2)}, u32[]{:S(2)}) %all-to-all-start) | async-done | bytes 12582944 | tf_op jit(solution)/shard_map/all_to_all | solution.py:92
  385.7 5.6 all-to-all-start.2
  391.3 10.7 fusion.8
  402.0 9.7 fusion.10
  411.7 251.5 %all-to-all-done.2 = bf16[8,4,96,2048]{3,2,1,0:T(8,128)(2,1)} async-done(((bf16[8,4,96,2048]{3,2,1,0:T(8,128)(2,1)}), bf16[8,4,96,2048]{3,2,1,0:T(8,128)(2,1)}, u32[]{:S(2)}, u32[]{:S(2)}) %all-to-all-start.2) | async-done | bytes 12582944 | tf_op jit(solution)/shard_map/all_to_all | solution.py:92
  663.2 10.0 fusion.32
  673.2 6.3 convert_bitcast_fusion
  679.5 10.7 copy.245
  690.2 5.9 all-to-all-start.1
  696.1 12.1 fusion.26
  708.2 15.5 fusion.3
  723.7 10.8 copy.248
  734.5 233.2 %all-to-all-done.1 = bf16[8,4,96,2048]{3,2,1,0:T(8,128)(2,1)} async-done(((bf16[8,4,96,2048]{3,2,1,0:T(8,128)(2,1)}), bf16[8,4,96,2048]{3,2,1,0:T(8,128)(2,1)}, u32[]{:S(2)}, u32[]{:S(2)}) %all-to-all-start.1) | async-done | bytes 12582944 | tf_op jit(solution)/shard_map/all_to_all | solution.py:184
  967.7 5.4 all-to-all-start.3
  975.3 22.7 %gather_fusion = bf16[2048,2048]{1,0:T(8,128)(2,1)} fusion(bf16[3072,2048]{1,0:T(8,128)(2,1)} %bitcast.30, s32[2048]{0:T(1024)S(1)} %broadcast_clamp_fusion), kind=kCustom, calls=%fused_computation | custom fusion | bytes 16785408 | tf_op jit(solution)/shard_map/gather | solution.py:187
  997.9 9.2 fusion.1
  1007.2 6.1 psum.80
  1013.3 231.9 %all-to-all-done.3 = bf16[8,4,96,2048]{3,2,1,0:T(8,128)(2,1)} async-done(((bf16[8,4,96,2048]{3,2,1,0:T(8,128)(2,1)}), bf16[8,4,96,2048]{3,2,1,0:T(8,128)(2,1)}, u32[]{:S(2)}, u32[]{:S(2)}) %all-to-all-start.3) | async-done | bytes 12582944 | tf_op jit(solution)/shard_map/all_to_all | solution.py:225
  1245.2 22.7 %gather_fusion.1 = bf16[2048,2048]{1,0:T(8,128)(2,1)} fusion(bf16[3072,2048]{1,0:T(8,128)(2,1)} %bitcast.39, s32[2048]{0:T(1024)S(1)} %broadcast_clamp_fusion), kind=kCustom, calls=%fused_computation.1 | custom fusion | bytes 16785408 | tf_op jit(solution)/shard_map/gather | solution.py:229
  1267.9 11.1 bitcast_reduce_fusion
  1280.4 34.0 %all-reduce.13.cloned.1.call-done = bf16[256,2048]{1,0:T(8,128)(2,1)} async-done(((bf16[256,2048]{1,0:T(8,128)(2,1)}), bf16[256,2048]{1,0:T(8,128)(2,1)}) %all-reduce.13.cloned.1.call-update) | async-done | bytes 1048592 | tf_op jit(solution)/shard_map/psum | solution.py:232
  1331.2 2.1 copy.256
  1338.8 3.7 fusion.120
  1345.6 4.3 convolution_convert_fusion
  1350.9 3.4 convolution_convert_fusion.1
  1355.8 9.9 fusion.21
  1365.7 10.5 convolution_bitcast_fusion
  1376.2 10.0 convolution_bitcast_fusion.1
  1387.5 5.9 all-reduce.5
  1393.4 52.1 %reduce-scatter.10.cloned.1.call-done = bf16[256,128]{1,0:T(8,128)(2,1)} async-done(((bf16[2048,128]{1,0:T(8,128)(2,1)}), bf16[256,128]{1,0:T(8,128)(2,1)}) %reduce-scatter.10.cloned.1.call-update) | async-done | bytes 65552 | tf_op jit(solution)/shard_map/reduce_scatter | solution.py:320
  1447.0 63.9 %reduce-scatter.8.cloned.1.call-done = bf16[256,128]{1,0:T(8,128)(2,1)} async-done(((bf16[2048,128]{1,0:T(8,128)(2,1)}), bf16[256,128]{1,0:T(8,128)(2,1)}) %reduce-scatter.8.cloned.1.call-update) | async-done | bytes 65552 | tf_op jit(solution)/shard_map/reduce_scatter | solution.py:317
  1512.4 52.4 %all-reduce.15.cloned.1.call-done = (bf16[256,2048]{1,0:T(8,128)(2,1)}, bf16[256,2048]{1,0:T(8,128)(2,1)}) async-done(((bf16[256,2048]{1,0:T(8,128)(2,1)}, bf16[256,2048]{1,0:T(8,128)(2,1)}), (bf16[256,2048]{1,0:T(8,128)(2,1)}, bf16[256,2048]{1,0:T(8,128)(2,1)})) %all-reduce.15.cloned.1.call-update) | async-done | bytes 2097168 | tf_op jit(solution)/shard_map/psum | solution.py:188
  1566.7 39.2 %all-reduce.4 = (f32[2048]{0:T(1024)}, f32[2048]{0:T(1024)}, f32[128]{0:T(128)}, f32[128]{0:T(128)}) all-reduce(f32[2048]{0:T(1024)S(1)} %get-tuple-element.20, f32[2048]{0:T(1024)S(1)} %get-tuple-element.16, bf16[128]{0:T(256)(128)(2,1)S(1)} %get-tuple-element.28, ...), channel_id=1, replica_groups=mesh['exp'=8,'tp'=4] {'exp'}, use_global_device_ids=true, to_apply=%region_29.30 | all-reduce | flops 4352 | bytes 34304 | tf_op jit(solution)/shard_map/psum | solution.py:330
  1605.9 5.3 fusion.44
  1611.2 46.1 %reduce-scatter.12.cloned.1.call-done = bf16[256,1024]{1,0:T(8,128)(2,1)} async-done(((bf16[2048,1024]{1,0:T(8,128)(2,1)}), bf16[256,1024]{1,0:T(8,128)(2,1)}) %reduce-scatter.12.cloned.1.call-update) | async-done | bytes 524304 | tf_op jit(solution)/shard_map/reduce_scatter | solution.py:323
  1657.3 2.1 convert_element_type.282
  1659.4 89.4 %reduce-scatter.6.cloned.1.call-done = bf16[256,1024]{1,0:T(8,128)(2,1)} async-done(((bf16[2048,1024]{1,0:T(8,128)(2,1)}), bf16[256,1024]{1,0:T(8,128)(2,1)}) %reduce-scatter.6.cloned.1.call-update) | async-done | bytes 524304 | tf_op jit(solution)/shard_map/reduce_scatter | solution.py:314
  1748.9 2.1 convert_element_type.276
  (269 shorter events, 61.0 us)
Async XLA Ops:
  7.2 656.0 %copy-start = (bf16[4,192,2048]{2,1,0:T(8,128)(2,1)S(1)}, bf16[4,192,2048]{2,1,0:T(8,128)(2,1)}, u32[]{:S(2)}) copy-start(bf16[4,192,2048]{2,1,0:T(8,128)(2,1)} %param.31) | copy-start | bytes 9437188
  7.2 7.2 copy-start.49
  7.2 75.7 %all-reduce.11.cloned.1.call-start = ((), (), s32[]{:S(2)}) async-start(), calls=%async_computation.9 | async-start | bytes 4194304 | tf_op jit(solution)/shard_map/psum | solution.py:159
  7.3 7.2 copy-start.4
  7.3 7.2 copy-start.38
  7.3 8.5 copy-start.73
  8.1 7.6 copy-start.67
  11.8 5.0 copy-start.63
  11.8 3.9 copy-start.71
  11.8 5.0 copy-start.83
  15.6 5.7 copy-start.34
  15.6 5.7 copy-start.36
  49.5 36.9 %copy-start.53 = (f32[2048]{0:T(1024)S(1)}, f32[2048]{0:T(1024)}, u32[]{:S(2)}) copy-start(f32[2048]{0:T(1024)} %param.21) | copy-start | bytes 24580
  85.7 21.5 %copy-start.65 = (f32[256]{0:T(256)}, f32[256]{0:T(256)S(1)}, u32[]{:S(2)}) copy-start(f32[256]{0:T(256)S(1)} %get-tuple-element.50) | copy-start | bytes 3076
  107.2 278.5 %all-to-all-start = ((bf16[8,4,96,2048]{3,2,1,0:T(8,128)(2,1)}), bf16[8,4,96,2048]{3,2,1,0:T(8,128)(2,1)}, u32[]{:S(2)}, u32[]{:S(2)}) async-start(bf16[8,4,96,2048]{3,2,1,0:T(8,128)(2,1)} %bitcast.256), calls=%async_computation | async-start | bytes 25165824 | tf_op jit(solution)/shard_map/all_to_all | solution.py:92
  385.7 277.5 %all-to-all-start.2 = ((bf16[8,4,96,2048]{3,2,1,0:T(8,128)(2,1)}), bf16[8,4,96,2048]{3,2,1,0:T(8,128)(2,1)}, u32[]{:S(2)}, u32[]{:S(2)}) async-start(bf16[8,4,96,2048]{3,2,1,0:T(8,128)(2,1)} %bitcast.257), calls=%async_computation.2 | async-start | bytes 25165824 | tf_op jit(solution)/shard_map/all_to_all | solution.py:92
  391.3 10.7 copy-start.26
  673.2 6.3 copy-start.30
  690.2 5.9 copy-start.16
  690.2 277.5 %all-to-all-start.1 = ((bf16[8,4,96,2048]{3,2,1,0:T(8,128)(2,1)}), bf16[8,4,96,2048]{3,2,1,0:T(8,128)(2,1)}, u32[]{:S(2)}, u32[]{:S(2)}) async-start(bf16[8,4,96,2048]{3,2,1,0:T(8,128)(2,1)} %copy.245), calls=%async_computation.1 | async-start | bytes 25165824 | tf_op jit(solution)/shard_map/all_to_all | solution.py:184
  696.1 12.1 copy-start.18
  734.5 238.6 %copy-start.56 = (f32[8,256]{1,0:T(8,128)S(1)}, f32[8,256]{1,0:T(8,128)}, u32[]{:S(2)}) copy-start(f32[8,256]{1,0:T(8,128)} %copy-done.55) | copy-start | bytes 24580
  734.5 238.6 %copy-start.62 = (f32[8,256]{1,0:T(8,128)S(1)}, f32[8,256]{1,0:T(8,128)}, u32[]{:S(2)}) copy-start(f32[8,256]{1,0:T(8,128)} %copy-done.61) | copy-start | bytes 24580
  734.5 238.7 %copy-start.7 = (f32[1,8,256,256]{2,3,1,0:T(8,128)S(1)}, f32[1,8,256,256]{2,3,1,0:T(8,128)}, u32[]{:S(2)}) copy-start(f32[1,8,256,256]{2,3,1,0:T(8,128)} %copy-done.6) | copy-start | bytes 6291460
  967.7 277.5 %all-to-all-start.3 = ((bf16[8,4,96,2048]{3,2,1,0:T(8,128)(2,1)}), bf16[8,4,96,2048]{3,2,1,0:T(8,128)(2,1)}, u32[]{:S(2)}, u32[]{:S(2)}) async-start(bf16[8,4,96,2048]{3,2,1,0:T(8,128)(2,1)} %copy.248), calls=%async_computation.3 | async-start | bytes 25165824 | tf_op jit(solution)/shard_map/all_to_all | solution.py:225
  973.1 341.4 %all-reduce.13.cloned.1.call-start = ((), (), s32[]{:S(2)}) async-start(), calls=%async_computation.10 | async-start | bytes 2097152 | tf_op jit(solution)/shard_map/psum | solution.py:232
  975.3 22.7 %copy-start.13 = (f32[256,2048]{1,0:T(8,128)S(1)}, f32[256,2048]{1,0:T(8,128)}, u32[]{:S(2)}) copy-start(f32[256,2048]{1,0:T(8,128)} %convert_element_type.243) | copy-start | bytes 6291460
  1267.9 11.3 copy-start.15
  1279.0 35.4 %copy-start.3 = (f32[256,2048]{1,0:T(8,128)S(1)}, f32[256,2048]{1,0:T(8,128)}, u32[]{:S(2)}) copy-start(f32[256,2048]{1,0:T(8,128)} %copy-done.2) | copy-start | bytes 6291460
  1279.0 35.4 %copy-start.42 = (bf16[2048,32]{0,1:T(8,128)(2,1)S(1)}, bf16[2048,32]{0,1:T(8,128)(2,1)}, u32[]{:S(2)}) copy-start(bf16[2048,32]{0,1:T(8,128)(2,1)} %param.28) | copy-start | bytes 393220
  1279.0 35.4 %copy-start.54 = (f32[2048]{0:T(1024)S(1)}, f32[2048]{0:T(1024)}, u32[]{:S(2)}) copy-start(f32[2048]{0:T(1024)} %param.21) | copy-start | bytes 24580
  1279.1 35.4 %copy-start.66 = (f32[256]{0:T(256)S(1)}, f32[256]{0:T(256)}, u32[]{:S(2)}) copy-start(f32[256]{0:T(256)} %copy-done.65) | copy-start | bytes 3076
  1279.1 107.1 %reduce-scatter.14.cloned.1.call-start = ((), (), s32[]{:S(2)}) async-start(), calls=%async_computation.15 | async-start | bytes 147456 | tf_op jit(solution)/shard_map/reduce_scatter | solution.py:326
  1280.2 36.4 %copy-start.25 = (bf16[256,2048]{1,0:T(8,128)(2,1)S(1)}, bf16[256,2048]{1,0:T(8,128)(2,1)}, u32[]{:S(2)}) copy-start(bf16[256,2048]{1,0:T(8,128)(2,1)} %param.17) | copy-start | bytes 3145732
  1280.2 36.4 %copy-start.78 = (f32[256]{0:T(256)S(1)}, f32[256]{0:T(256)}, u32[]{:S(2)}) copy-start(f32[256]{0:T(256)} %get-tuple-element.49) | copy-start | bytes 3076
  1280.2 165.3 %reduce-scatter.10.cloned.1.call-start = ((), (), s32[]{:S(2)}) async-start(), calls=%async_computation.13 | async-start | bytes 589824 | tf_op jit(solution)/shard_map/reduce_scatter | solution.py:320
  1331.2 4.0 copy-start.5
  1331.2 4.0 copy-start.50
  1331.2 4.0 copy-start.64
  1333.4 3.9 copy-start.80
  1336.7 174.2 %reduce-scatter.8.cloned.1.call-start = ((), (), s32[]{:S(2)}) async-start(), calls=%async_computation.12 | async-start | bytes 589824 | tf_op jit(solution)/shard_map/reduce_scatter | solution.py:317
  1338.8 226.0 %all-reduce.15.cloned.1.call-start = ((), (), s32[]{:S(2)}) async-start(), calls=%async_computation.16 | async-start | bytes 4194304 | tf_op jit(solution)/shard_map/psum | solution.py:188
  1338.8 3.7 copy-start.39
  1345.1 312.2 %reduce-scatter.12.cloned.1.call-start = ((), (), s32[]{:S(2)}) async-start(), calls=%async_computation.14 | async-start | bytes 4718592 | tf_op jit(solution)/shard_map/reduce_scatter | solution.py:323
  1349.9 398.9 %reduce-scatter.6.cloned.1.call-start = ((), (), s32[]{:S(2)}) async-start(), calls=%async_computation.11 | async-start | bytes 4718592 | tf_op jit(solution)/shard_map/reduce_scatter | solution.py:314
  1365.7 10.5 copy-start.17
  1386.2 219.7 %copy-start.77 = (f32[256]{0:T(256)S(1)}, f32[256]{0:T(256)}, u32[]{:S(2)}) copy-start(f32[256]{0:T(256)} %get-tuple-element.47) | copy-start | bytes 3076
  1605.9 145.1 %copy-start.1 = (bf16[4,192,2048]{2,1,0:T(8,128)(2,1)S(1)}, bf16[4,192,2048]{2,1,0:T(8,128)(2,1)}, u32[]{:S(2)}) copy-start(bf16[4,192,2048]{2,1,0:T(8,128)(2,1)} %param.31) | copy-start | bytes 9437188
  (48 other events, 85.8 us)
Sparse Core Ops, SparseCore 0:
  28.7 54.0 all-reduce.10
  1279.2 35.2 all-reduce.12
  1317.8 62.8 reduce-scatter.13
  1383.8 61.5 reduce-scatter.9
  1449.3 61.5 reduce-scatter.7
  1514.3 50.4 all-reduce.14
  1568.4 88.8 reduce-scatter.11
  1660.9 87.9 reduce-scatter.5
where the time goes:
time: 1770 us; the launch traced here: 1760 us
  waiting for transfers between devices  1320 us (75%)
  matrix products  129 us (7%)
  local copies, waits for them, and re-layouts  124 us (7%)
  other arithmetic  95.6 us (5%)
  blocking collectives  51.2 us (3%)
  starting transfers between devices  23.3 us (1%)
    all_to_all x2, waiting for transfers between devices, to_owner(): lax.all_to_all(buffer_rows, 'exp', split_axis=0, concat_axis=0, tiled=True)  483 us
    all_to_all x1, waiting for transfers between devices, body(): lax.all_to_all(expert_part, 'exp', split_axis=0, concat_axis=0, tiled=True)  233 us
    all_to_all x1, waiting for transfers between devices, body(): lax.all_to_all(expert_input_grad, 'exp', split_axis=0, concat_axis=0, til...  232 us
    reduce_scatter x1, waiting for transfers between devices, body(): lax.psum_scatter(query_part.astype(jnp.bfloat16), 'exp', scatter_dimensio...  89.4 us
    reduce_scatter x1, waiting for transfers between devices, body(): lax.psum_scatter(key_part.astype(jnp.bfloat16), 'exp', scatter_dimension=...  63.9 us
    psum x1, waiting for transfers between devices, body(): lax.psum(jnp.sum(gates[..., None] * picked, 1).astype(jnp.bfloat16), 'tp')  52.4 us
    reduce_scatter x1, waiting for transfers between devices, body(): lax.psum_scatter(value_part.astype(jnp.bfloat16), 'exp', scatter_dimensio...  52.1 us
    reduce_scatter x1, waiting for transfers between devices, body(): lax.psum_scatter(out_part.astype(jnp.bfloat16), 'exp', scatter_dimension=...  46.1 us
  transfers between devices with their start and end apart: 12, of which 11 were waited for; matrix products, arithmetic and copies ran while one was open for 13% of the time, Pallas kernels for 0%

commit v1 on v0

v1 whole, which is shorter than its diff:
```python
import jax
import jax.numpy as jnp
from jax import lax
from jax.sharding import PartitionSpec as P

HEAD_DIMENSION = 128
EPSILON = 1e-06
ROPE_BASE = 1000000.0
MASKED = -1e30
F32 = jnp.float32
BF = jnp.bfloat16
LAST = (((1,), (1,)), ((), ()))
FIRST = (((0,), (0,)), ((), ()))


def dot(a, b, dims=(((1,), (0,)), ((), ()))):
    return lax.dot_general(a, b, dims, preferred_element_type=F32)


def rotate_normed(pre_proj, gain_vec, cosine, sine):
    normed = (
        pre_proj * lax.rsqrt(jnp.mean(pre_proj * pre_proj, -1, keepdims=True) + EPSILON) * gain_vec
    )
    half_dim = HEAD_DIMENSION // 2
    first_half = normed[..., :half_dim]
    second_half = normed[..., half_dim:]
    return jnp.concatenate(
        [first_half * cosine - second_half * sine, second_half * cosine + first_half * sine], -1
    )


def body(
    tokens,
    cotangent,
    seq_start,
    routes,
    norm1_gain,
    norm2_gain,
    q_gain,
    k_gain,
    query_matrix,
    key_matrix,
    value_matrix,
    output_matrix,
    w_router,
    w_gate,
    w_up,
    w_down,
):
    rows, width = tokens.shape
    groups = key_matrix.shape[1] // HEAD_DIMENSION
    heads = query_matrix.shape[1] // HEAD_DIMENSION
    repeats = heads // groups
    all_experts = w_router.shape[1]
    local, _, share = w_gate.shape
    n_tp = lax.axis_size("tp")
    quarter = rows // n_tp
    t_id = lax.axis_index("tp")
    e_id = lax.axis_index("exp")
    both = ("exp", "tp")

    def my_rows(a):
        return lax.dynamic_slice_in_dim(a, t_id * quarter, quarter, 0)

    def gather_all(a):
        return lax.all_gather(a, both, axis=0, tiled=True)

    gy_all = gather_all(my_rows(cotangent))
    routes_all = lax.all_gather(routes, "exp", axis=0, tiled=True)

    w_gu = jnp.concatenate(
        [
            jnp.transpose(w_gate, (1, 0, 2)).reshape(width, local * share),
            jnp.transpose(w_up, (1, 0, 2)).reshape(width, local * share),
        ],
        1,
    )
    w_dn = w_down.reshape(local * share, width)

    resid = tokens.astype(F32)
    scale_one = lax.rsqrt(jnp.mean(resid * resid, -1, keepdims=True) + EPSILON)
    normed_one = (resid * scale_one * norm1_gain).astype(BF)
    half_dim = HEAD_DIMENSION // 2
    freqs = ROPE_BASE ** (-(jnp.arange(half_dim).astype(F32) * 2.0 / HEAD_DIMENSION))
    angles = (jnp.arange(rows) - seq_start).astype(F32)[:, None] * freqs
    cosine, sine = jnp.cos(angles), jnp.sin(angles)
    q_pre = dot(normed_one, query_matrix).reshape(rows, heads, HEAD_DIMENSION)
    q_pre = jnp.transpose(q_pre, (1, 0, 2)).reshape(groups, repeats, rows, HEAD_DIMENSION)
    k_pre = dot(normed_one, key_matrix).reshape(rows, groups, HEAD_DIMENSION)
    k_pre = jnp.transpose(k_pre, (1, 0, 2))
    value = dot(normed_one, value_matrix).astype(BF).reshape(rows, groups, HEAD_DIMENSION)
    value = jnp.transpose(value, (1, 0, 2))
    rot = lambda pre, gain: rotate_normed(pre, gain, cosine, sine)
    q_rot, q_back = jax.vjp(rot, q_pre, q_gain)
    k_rot, k_back = jax.vjp(rot, k_pre, k_gain)
    q_bf = q_rot.astype(BF)
    k_bf = k_rot.astype(BF)
    ids = jnp.arange(rows)
    allowed = (ids[None, :] <= ids[:, None]) & (seq_start[None, :] == seq_start[:, None])
    scores = jnp.einsum("grid,gjd->grij", q_bf, k_bf, preferred_element_type=F32)
    scores = jnp.where(allowed, scores * HEAD_DIMENSION ** (-0.5), MASKED)
    peak = jnp.max(scores, -1, keepdims=True)
    weights = jnp.exp(scores - peak)
    probs = weights / jnp.sum(weights, -1, keepdims=True)
    probs_bf = probs.astype(BF)
    attended = jnp.einsum("grij,gjd->grid", probs_bf, value, preferred_element_type=F32).astype(BF)
    att_flat = jnp.transpose(attended.reshape(heads, rows, HEAD_DIMENSION), (1, 0, 2)).reshape(
        rows, heads * HEAD_DIMENSION
    )
    attn_part = dot(att_flat, output_matrix, LAST)
    after = my_rows(tokens).astype(F32) + lax.psum_scatter(
        attn_part, "tp", scatter_dimension=0, tiled=True
    )
    scale_two = lax.rsqrt(jnp.mean(after * after, -1, keepdims=True) + EPSILON)
    normed_two = (after * scale_two * norm2_gain).astype(BF)
    x_all = gather_all(normed_two)

    logits = dot(x_all, w_router)
    named = jnp.any(routes_all[:, :, None] == jnp.arange(all_experts)[None, None, :], 1)
    logits = jnp.where(named, logits, MASKED)
    gexp = jnp.where(named, jnp.exp(logits - jnp.max(logits, -1, keepdims=True)), 0.0)
    gates = gexp / jnp.sum(gexp, -1, keepdims=True)
    mine = lax.dynamic_slice_in_dim(gates, e_id * local, local, 1)
    wide = jnp.repeat(mine, share, axis=1)
    pre = dot(x_all, w_gu)
    gate_pre, up_pre = pre[:, : local * share], pre[:, local * share :]
    g_hidden = dot(gy_all, w_dn, LAST)
    sig = jax.nn.sigmoid(gate_pre)
    silu = gate_pre * sig
    hidden = silu * up_pre
    gates_part = jnp.sum((hidden * g_hidden).reshape(-1, local, share), -1)
    gated_hidden = (wide * hidden).astype(BF)
    mix_part = dot(gated_hidden, w_dn).astype(BF)
    grad_hidden = wide * g_hidden
    grad_gate_pre = grad_hidden * up_pre * sig * (1.0 + gate_pre * (1.0 - sig))
    grad_up_pre = grad_hidden * silu
    grad_pre = jnp.concatenate([grad_gate_pre, grad_up_pre], 1).astype(BF)
    dx_part = dot(grad_pre, w_gu, LAST).astype(BF)

    gg = lax.all_to_all(gates_part, "exp", split_axis=0, concat_axis=1, tiled=True)
    grad_gates = lax.psum_scatter(gg, "tp", scatter_dimension=0, tiled=True)
    my_gates = lax.dynamic_slice_in_dim(gates, (e_id * n_tp + t_id) * quarter, quarter, 0)
    grad_logits = (
        my_gates * (grad_gates - jnp.sum(my_gates * grad_gates, -1, keepdims=True))
    ).astype(BF)
    glog_all = gather_all(grad_logits)

    dx = lax.psum_scatter(dx_part, both, scatter_dimension=0, tiled=True).astype(F32)
    mixture = lax.psum_scatter(mix_part, both, scatter_dimension=0, tiled=True).astype(F32)
    layer_out = lax.all_gather((after + mixture).astype(BF), "tp", axis=0, tiled=True)

    grad_n2 = dx + dot(grad_logits, w_router, LAST)
    gain2 = grad_n2 * norm2_gain
    norm2_part = jnp.sum(grad_n2 * after * scale_two, 0)
    grad_resid = (
        my_rows(cotangent).astype(F32)
        + scale_two * gain2
        - after * scale_two**3 * jnp.mean(gain2 * after, -1, keepdims=True)
    )
    grad_resid_bf = lax.all_gather(grad_resid.astype(BF), "tp", axis=0, tiled=True)

    out_part = dot(grad_resid_bf, att_flat, FIRST)
    grad_att = dot(grad_resid_bf, output_matrix).astype(BF).reshape(rows, heads, HEAD_DIMENSION)
    grad_att = jnp.transpose(grad_att, (1, 0, 2)).reshape(groups, repeats, rows, HEAD_DIMENSION)
    grad_value = jnp.einsum("grij,grid->gjd", probs_bf, grad_att, preferred_element_type=F32)
    grad_probs = jnp.einsum("grid,gjd->grij", grad_att, value, preferred_element_type=F32)
    delta = jnp.sum(grad_att.astype(F32) * attended.astype(F32), -1, keepdims=True)
    grad_scores = (probs * (grad_probs - delta) ).astype(BF)
    scale = HEAD_DIMENSION ** (-0.5)
    grad_q = jnp.einsum("grij,gjd->grid", grad_scores, k_bf, preferred_element_type=F32) * scale
    grad_k = jnp.einsum("grij,grid->gjd", grad_scores, q_bf, preferred_element_type=F32) * scale
    gq_pre, q_gain_part = q_back(grad_q)
    gk_pre, k_gain_part = k_back(grad_k)
    flat = lambda a: jnp.transpose(a.reshape(-1, rows, HEAD_DIMENSION), (1, 0, 2)).reshape(rows, -1)
    gqkv = jnp.concatenate(
        [flat(gq_pre).astype(BF), flat(gk_pre).astype(BF), flat(grad_value).astype(BF)], 1
    )
    nq, nk = query_matrix.shape[1], key_matrix.shape[1]
    input_part = (
        dot(gqkv[:, :nq], query_matrix, LAST)
        + dot(gqkv[:, nq : nq + nk], key_matrix, LAST)
        + dot(gqkv[:, nq + nk :], value_matrix, LAST)
    )
    qkv_part = dot(normed_one, gqkv, FIRST)
    grad_n1 = lax.psum_scatter(
        input_part.astype(BF), "tp", scatter_dimension=0, tiled=True
    ).astype(F32)
    my_resid = my_rows(tokens).astype(F32)
    my_scale = my_rows(scale_one)
    gain1 = grad_n1 * norm1_gain
    norm1_part = jnp.sum(grad_n1 * my_resid * my_scale, 0)
    grad_tokens = (
        grad_resid
        + my_scale * gain1
        - my_resid * my_scale**3 * jnp.mean(gain1 * my_resid, -1, keepdims=True)
    ).astype(BF)
    grad_tokens = lax.all_gather(grad_tokens, "tp", axis=0, tiled=True)

    grad_out = lax.psum_scatter(
        out_part.astype(BF), "exp", scatter_dimension=0, tiled=True
    ).astype(F32)
    qkv = lax.psum_scatter(qkv_part.astype(BF), "exp", scatter_dimension=0, tiled=True).astype(F32)
    cols = width // lax.axis_size("exp")
    x_cols = lax.dynamic_slice_in_dim(x_all, e_id * cols, cols, 1)
    grad_router = dot(x_cols, glog_all, FIRST)
    small = jnp.concatenate([norm1_part, norm2_part, q_gain_part, k_gain_part])
    small = lax.psum(small, both)

    w_grad = dot(x_all, grad_pre, FIRST)
    down_grad = dot(gated_hidden, gy_all, FIRST)
    unfold = lambda a: jnp.transpose(a.reshape(width, local, share), (1, 0, 2))
    return (
        layer_out,
        grad_tokens,
        small[:width],
        small[width : 2 * width],
        small[2 * width : 2 * width + HEAD_DIMENSION],
        small[2 * width + HEAD_DIMENSION :],
        qkv[:, :nq],
        qkv[:, nq : nq + nk],
        qkv[:, nq + nk :],
        grad_out,
        grad_router,
        unfold(w_grad[:, : local * share]),
        unfold(w_grad[:, local * share :]),
        down_grad.reshape(local, share, width),
    )


def solution(mesh):
    e, t = "exp", "tp"
    return jax.shard_map(
        body,
        mesh=mesh,
        in_specs=(
            P(e, None), P(e, None), P(e), P(e, None), P(), P(), P(), P(),
            P(None, t), P(None, t), P(None, t), P(None, t), P(),
            P(e, None, t), P(e, None, t), P(e, t, None),
        ),
        out_specs=(
            P(e, None), P(e, None), P(), P(), P(), P(),
            P(e, t), P(e, t), P(e, t), P(e, t), P(e, None),
            P(e, None, t), P(e, None, t), P(e, t, None),
        ),
        check_vma=False,
    )
```

time: 1770 us -> 893 us (0.50)
  waiting for transfers between devices: 1320 us -> 545 us
  local copies, waits for them, and re-layouts: 124 us -> 31.9 us
  blocking collectives: 51.2 us -> 124 us
  other arithmetic: 95.6 us -> 29 us
  starting transfers between devices: 23.3 us -> 1.13 us
    all_to_all x4 -> x0, waiting for transfers between devices: 948 us -> none  [the longest x2 483 us: to_owner(): lax.all_to_all(buffer_rows, 'exp', split_axis=0, concat_axis=0, tiled=True)]
    reduce_scatter x5 -> x6, waiting for transfers between devices: 252 us -> 433 us  [the longest x1 146 us: body(): lax.psum_scatter(mix_part, both, scatter_dimension=0, tiled=True)]
    psum x3 -> x0, waiting for transfers between devices: 120 us -> none  [the longest x1 52.4 us: body(): lax.psum(jnp.sum(gates[..., None] * picked, 1).astype(jnp.bfloat16), 'tp')]
    all_gather x0 -> x5, waiting for transfers between devices: none -> 111 us  [the longest x2 98.7 us: gather_all(): return lax.all_gather(a, both, axis=0, tiled=True)]
    all_gather x0 -> x2, blocking collectives: none -> 74.4 us  [the longest x1 43.2 us: gather_all(): return lax.all_gather(a, both, axis=0, tiled=True)]
    gather x7 -> x0, local copies, waits for them, and re-layouts: 62.6 us -> none  [the longest x1 22.7 us: body(): grads_back[places].astype(jnp.float32).reshape(tok_rows, TOPK, model_width)]
    convert_element_type x4 -> x2, local copies, waits for them, and re-layouts: 24.8 us -> 1.46 us  [the longest x1 1.24 us: body(): dot(grad_resid_bf, output_matrix).astype(BF)]
    all_to_all x4 -> x0, starting transfers between devices: 22.5 us -> none  [the longest x2 11.3 us: to_owner(): lax.all_to_all(buffer_rows, 'exp', split_axis=0, concat_axis=0, tiled=True)]
  transfers between devices with their start and end apart: 12 -> 12, of which waited for: 11 -> 8; matrix products, arithmetic and copies ran while one was open for 13% -> 13% of each run, Pallas kernels for 0% -> 0%
where the time goes in v1:
time: 893 us; the launch traced here: 887 us
  waiting for transfers between devices  545 us (61%)
  matrix products  141 us (16%)
  blocking collectives  124 us (14%)
  local copies, waits for them, and re-layouts  31.9 us (4%)
  other arithmetic  29 us (3%)
  between operations  15.5 us (2%)
    reduce_scatter x1, waiting for transfers between devices, body(): lax.psum_scatter(mix_part, both, scatter_dimension=0, tiled=True)  146 us
    reduce_scatter x1, waiting for transfers between devices, body(): lax.psum_scatter(dx_part, both, scatter_dimension=0, tiled=True).astype(F32)  135 us
    dot_general x19, matrix products, dot(): return lax.dot_general(a, b, dims, preferred_element_type=F32)  131 us
    all_gather x2, waiting for transfers between devices, gather_all(): return lax.all_gather(a, both, axis=0, tiled=True)  98.7 us
    reduce_scatter x1, waiting for transfers between devices, body(): lax.psum_scatter(qkv_part.astype(BF), 'exp', scatter_dimension=0, tiled=T...  93.5 us
    all_gather x1, blocking collectives, gather_all(): return lax.all_gather(a, both, axis=0, tiled=True)  43.2 us
    psum x1, blocking collectives, body(): small = lax.psum(small, both)  38.9 us
    reduce_scatter x1, waiting for transfers between devices, body(): lax.psum_scatter(attn_part, 'tp', scatter_dimension=0, tiled=True)  34 us
  transfers between devices with their start and end apart: 12, of which 8 were waited for; matrix products, arithmetic and copies ran while one was open for 13% of the time, Pallas kernels for 0%

profile of v1, /device:TPU:0, one launch (start us, length us, event | category | flops | bytes accessed | tf_op | source)
XLA Modules:
  0.0 887.2 jit_solution(11220564820233500208)
XLA Ops:
  7.3 1.6 fusion.48
  9.5 1.5 fusion.7
  11.1 2.0 multiply_reduce_fusion.4
  15.3 3.9 convolution_bitcast_fusion
  21.2 1.4 fusion.45
  22.6 4.1 fusion.98
  26.7 1.9 fusion.31
  30.8 2.6 fusion.100
  33.5 34.0 %reduce-scatter.10.cloned.1.call-done = f32[64,2048]{1,0:T(8,128)} async-done(((f32[256,2048]{1,0:T(8,128)}), f32[64,2048]{1,0:T(8,128)}) %reduce-scatter.10.cloned.1.call-update) | async-done | bytes 524304 | tf_op jit(solution)/shard_map/reduce_scatter | solution.py:111
  67.5 1.3 multiply_reduce_fusion.3
  70.5 1.7 constant_dynamic-slice_fusion
  72.3 31.3 %all_gather.21 = s32[2048,8]{0,1:T(8,128)S(1)} all-gather(s32[256,8]{0,1:T(8,128)S(1)} %copy-done.47), channel_id=1, replica_groups=mesh['exp'=8,'tp'=4] {'exp'}, dimensions={0}, use_global_device_ids=true | all-gather | bytes 73728 | tf_op jit(solution)/shard_map/all_gather | solution.py:69
  103.9 44.2 %all-gather.7.cloned.1.call-done = bf16[2048,2048]{1,0:T(8,128)(2,1)} async-done(((bf16[64,2048]{1,0:T(8,128)(2,1)}), bf16[2048,2048]{1,0:T(8,128)(2,1)}) %all-gather.7.cloned.1.call-update) | async-done | bytes 8388624 | tf_op jit(solution)/shard_map/all_gather | solution.py:66
  148.1 6.1 fusion.99
  155.1 17.6 %fusion.4 = f32[2048,1536]{0,1:T(8,128)} fusion(bf16[2048,2048]{1,0:T(8,128)(2,1)S(1)} %copy-done.2, bf16[2048,768]{0,1:T(8,128)(2,1)S(1)} %bitcast.217, bf16[2048,768]{0,1:T(8,128)(2,1)} %bitcast.218), kind=kOutput, calls=%fused_computation.15 | convolution fusion | flops 12897484800 | bytes 27262976 | tf_op jit(solution)/shard_map/dot_general | solution.py:17
  172.7 54.5 %all-gather.11.cloned.1.call-done = bf16[2048,2048]{1,0:T(8,128)(2,1)} async-done(((bf16[64,2048]{1,0:T(8,128)(2,1)}), bf16[2048,2048]{1,0:T(8,128)(2,1)}) %all-gather.11.cloned.1.call-update) | async-done | bytes 8388624 | tf_op jit(solution)/shard_map/all_gather | solution.py:66
  227.2 16.9 %multiply_convert_fusion.1 = (bf16[2048,768]{0,1:T(8,128)(2,1)}, bf16[2048,768]{0,1:T(8,128)(2,1)}, f32[2048,768]{0,1:T(8,128)}, bf16[2048,768]{0,1:T(8,128)(2,1)}) fusion(f32[2048,1536]{0,1:T(8,128)} %fusion.4, f32[2048,4]{0,1:T(4,128)S(1)} %constant_dynamic-slice_fusion.1, bf16[2048,2048]{1,0:T(8,128)(2,1)} %all-gather.11.cloned.1.call-done, ...), kind=kOutput, calls=%fused_computation.10 | convolution fusion | flops 6470762496 | bytes 39878656 | tf_op jit(solution)/shard_map/dot_general | solution.py:17
  244.1 3.2 reduce_sum.175
  247.3 10.6 %all_to_all.19 = f32[8,256,4]{1,2,0:T(4,128)S(1)} all-to-all(f32[8,256,4]{1,2,0:T(4,128)S(1)} %bitcast.213), channel_id=1, replica_groups=mesh['exp'=8,'tp'=4] {'exp'}, dimensions={0} | all-to-all | bytes 65536 | tf_op jit(solution)/shard_map/all_to_all | solution.py:140
  259.0 19.5 %convolution_convert_fusion.1 = bf16[2048,2048]{1,0:T(8,128)(2,1)} fusion(bf16[2048,768]{0,1:T(8,128)(2,1)} %get-tuple-element.29, bf16[2048,768]{0,1:T(8,128)(2,1)} %get-tuple-element.28, bf16[2048,768]{0,1:T(8,128)(2,1)} %bitcast.216, bf16[2048,768]{0,1:T(8,128)(2,1)} %bitcast.219), kind=kOutput, calls=%fused_computation.4 | convolution fusion | flops 12914262016 | bytes 20971520 | tf_op jit(solution)/shard_map/dot_general | solution.py:17
  278.5 11.0 %convolution_convert_fusion.2 = bf16[2048,2048]{1,0:T(8,128)(2,1)} fusion(bf16[2048,768]{0,1:T(8,128)(2,1)} %get-tuple-element.31, bf16[768,2048]{1,0:T(8,128)(2,1)S(1)} %bitcast.202), kind=kOutput, calls=%fused_computation.5 | convolution fusion | flops 6446645248 | bytes 14680064 | tf_op jit(solution)/shard_map/dot_general | solution.py:17
  292.2 135.2 %reduce-scatter.14.cloned.1.call-done = bf16[64,2048]{1,0:T(8,128)(2,1)} async-done(((bf16[2048,2048]{1,0:T(8,128)(2,1)}), bf16[64,2048]{1,0:T(8,128)(2,1)}) %reduce-scatter.14.cloned.1.call-update) | async-done | bytes 262160 | tf_op jit(solution)/shard_map/reduce_scatter | solution.py:148
  427.4 1.9 multiply_reduce_fusion.1
  429.3 146.4 %reduce-scatter.12.cloned.1.call-done = bf16[64,2048]{1,0:T(8,128)(2,1)} async-done(((bf16[2048,2048]{1,0:T(8,128)(2,1)}), bf16[64,2048]{1,0:T(8,128)(2,1)}) %reduce-scatter.12.cloned.1.call-update) | async-done | bytes 262160 | tf_op jit(solution)/shard_map/reduce_scatter | solution.py:149
  575.7 2.3 fusion.93
  578.3 12.4 %all-gather.13.cloned.1.call-done = bf16[256,2048]{1,0:T(8,128)(2,1)} async-done(((bf16[64,2048]{1,0:T(8,128)(2,1)}), bf16[256,2048]{1,0:T(8,128)(2,1)}) %all-gather.13.cloned.1.call-update) | async-done | bytes 1048592 | tf_op jit(solution)/shard_map/all_gather | solution.py:160
  590.7 4.6 convolution_convert_fusion.5
  596.7 1.3 multiply_convert_fusion.2
  598.7 1.3 fusion.14
  600.0 1.5 fusion.15
  604.2 3.7 fusion.101
  609.1 1.4 fusion.5
  611.5 24.0 %reduce-scatter.16.cloned.1.call-done = bf16[64,2048]{1,0:T(8,128)(2,1)} async-done(((bf16[256,2048]{1,0:T(8,128)(2,1)}), bf16[64,2048]{1,0:T(8,128)(2,1)}) %reduce-scatter.16.cloned.1.call-update) | async-done | bytes 262160 | tf_op jit(solution)/shard_map/reduce_scatter | solution.py:185
  636.7 2.0 fusion.40
  638.8 4.3 convolution_convert_fusion.3
  644.2 4.0 convolution_convert_fusion
  648.3 1.9 copy-done.15
  650.1 18.1 %fusion.3 = f32[2048,1536]{0,1:T(8,128)} fusion(bf16[2048,2048]{1,0:T(8,128)(2,1)} %all-gather.7.cloned.1.call-done, bf16[2048,768]{0,1:T(8,128)(2,1)} %get-tuple-element.29, bf16[2048,768]{0,1:T(8,128)(2,1)S(1)} %copy-done.15), kind=kOutput, calls=%fused_computation.14 | convolution fusion | flops 12897484800 | bytes 27262976 | tf_op jit(solution)/shard_map/dot_general | solution.py:17
  668.2 11.8 %fusion.94 = (f32[2048,768]{0,1:T(8,128)}, f32[2048,768]{0,1:T(8,128)}) fusion(f32[2048,1536]{0,1:T(8,128)} %fusion.3), kind=kLoop, calls=%fused_computation.171 | loop fusion | bytes 25165824 | tf_op jit(solution)/shard_map/slice | solution.py:225
  680.0 10.7 %fusion.102 = f32[768,2048]{1,0:T(8,128)} fusion(bf16[2048,768]{0,1:T(8,128)(2,1)S(1)} %copy-done.14, bf16[2048,2048]{1,0:T(8,128)(2,1)} %all-gather.11.cloned.1.call-done), kind=kOutput, calls=%fused_computation.179 | convolution fusion | flops 6442450944 | bytes 17825792 | tf_op jit(solution)/shard_map/dot_general | solution.py:17
  690.7 43.2 %all-gather = bf16[32,64,32]{1,2,0:T(8,128)(2,1)S(1)} all-gather(bf16[1,64,32]{1,2,0:T(8,128)(2,1)S(1)} %bitcast.215), channel_id=1, replica_groups=mesh['exp'=8,'tp'=4] {'exp','tp'}, dimensions={0}, use_global_device_ids=true | all-gather | bytes 135168 | tf_op jit(solution)/shard_map/all_gather | solution.py:66
  734.2 2.1 fusion.26
  736.4 38.9 %psum.7 = f32[4352]{0:T(1024)S(1)} all-reduce(f32[4352]{0:T(1024)S(1)} %pad_maximum_fusion.7), channel_id=1, replica_groups=mesh['exp'=8,'tp'=4] {'exp','tp'}, use_global_device_ids=true, to_apply=%region_25.26 | all-reduce | flops 4352 | bytes 34816 | tf_op jit(solution)/shard_map/psum | solution.py:207
  776.4 2.9 convert_element_type.171
  779.3 93.5 %reduce-scatter.18.cloned.1.call-done = bf16[256,1280]{1,0:T(8,128)(2,1)} async-done(((bf16[2048,1280]{1,0:T(8,128)(2,1)}), bf16[256,1280]{1,0:T(8,128)(2,1)}) %reduce-scatter.18.cloned.1.call-update) | async-done | bytes 655376 | tf_op jit(solution)/shard_map/reduce_scatter | solution.py:202
  872.8 2.2 slice.70
  875.0 1.6 fusion.95
  876.6 2.3 copy.116
  (193 shorter events, 25.1 us)
Async XLA Ops:
  7.2 220.0 %copy-start = (bf16[4,192,2048]{2,1,0:T(8,128)(2,1)S(1)}, bf16[4,192,2048]{2,1,0:T(8,128)(2,1)}, u32[]{:S(2)}) copy-start(bf16[4,192,2048]{2,1,0:T(8,128)(2,1)} %param.31) | copy-start | bytes 9437188
  7.2 60.3 %reduce-scatter.10.cloned.1.call-start = ((), (), s32[]{:S(2)}) async-start(), calls=%async_computation.8 | async-start | bytes 2621440 | tf_op jit(solution)/shard_map/reduce_scatter | solution.py:111
  7.3 7.7 copy-start.51
  9.5 5.4 copy-start.42
  11.1 8.6 copy-start.44
  14.2 7.0 copy-start.22
  15.3 5.0 copy-start.5
  15.3 5.0 copy-start.27
  15.3 5.0 copy-start.31
  15.3 5.5 copy-start.53
  20.8 7.9 copy-start.38
  26.7 4.1 copy-start.58
  30.8 38.8 %copy-start.32 = (f32[2048]{0:T(1024)S(1)}, f32[2048]{0:T(1024)}, u32[]{:S(2)}) copy-start(f32[2048]{0:T(1024)} %param.21) | copy-start | bytes 24580
  33.4 38.8 %copy-start.47 = (s32[256,8]{0,1:T(8,128)S(1)}, s32[256,8]{0,1:T(8,128)}, u32[]{:S(2)}) copy-start(s32[256,8]{0,1:T(8,128)} %param.19) | copy-start | bytes 24580
  33.5 114.6 %all-gather.7.cloned.1.call-start = ((), (), s32[]{:S(2)}) async-start(), calls=%async_computation.9 | async-start | bytes 8650752 | tf_op jit(solution)/shard_map/all_gather | solution.py:66
  70.5 156.7 %all-gather.11.cloned.1.call-start = ((), (), s32[]{:S(2)}) async-start(), calls=%async_computation.12 | async-start | bytes 8650752 | tf_op jit(solution)/shard_map/all_gather | solution.py:66
  72.2 217.4 %reduce-scatter.22.cloned.1.call-start = ((), (), s32[]{:S(2)}) async-start(), calls=%async_computation.19 | async-start | bytes 163840
  148.0 7.0 copy-start.2
  148.1 7.0 copy-start.59
  258.8 168.6 %reduce-scatter.14.cloned.1.call-start = ((), (), s32[]{:S(2)}) async-start(), calls=%async_computation.13 | async-start | bytes 8650752 | tf_op jit(solution)/shard_map/reduce_scatter | solution.py:148
  278.5 297.2 %reduce-scatter.12.cloned.1.call-start = ((), (), s32[]{:S(2)}) async-start(), calls=%async_computation.10 | async-start | bytes 8650752 | tf_op jit(solution)/shard_map/reduce_scatter | solution.py:149
  289.5 137.8 %copy-start.10 = (f32[64,2048]{1,0:T(8,128)S(1)}, f32[64,2048]{1,0:T(8,128)}, u32[]{:S(2)}) copy-start(f32[64,2048]{1,0:T(8,128)} %copy-done.9) | copy-start | bytes 1572868
  289.5 137.8 %copy-start.25 = (bf16[2048,32]{0,1:T(8,128)(2,1)S(1)}, bf16[2048,32]{0,1:T(8,128)(2,1)}, u32[]{:S(2)}) copy-start(bf16[2048,32]{0,1:T(8,128)(2,1)} %param.28) | copy-start | bytes 393220
  289.5 137.8 %copy-start.33 = (f32[2048]{0:T(1024)S(1)}, f32[2048]{0:T(1024)}, u32[]{:S(2)}) copy-start(f32[2048]{0:T(1024)} %param.21) | copy-start | bytes 24580
  289.5 137.8 %copy-start.49 = (f32[64]{0:T(128)S(1)}, f32[64]{0:T(128)}, u32[]{:S(2)}) copy-start(f32[64]{0:T(128)} %copy-done.48) | copy-start | bytes 772
  289.5 286.1 %copy-start.57 = (f32[64]{0:T(128)S(1)}, f32[64]{0:T(128)}, u32[]{:S(2)}) copy-start(f32[64]{0:T(128)} %get-tuple-element.51) | copy-start | bytes 772
  289.6 301.1 %all-gather.13.cloned.1.call-start = ((), (), s32[]{:S(2)}) async-start(), calls=%async_computation.14 | async-start | bytes 1310720 | tf_op jit(solution)/shard_map/all_gather | solution.py:160
  292.2 303.1 %copy-start.36 = (bf16[64,32]{0,1:T(8,128)(2,1)}, bf16[64,32]{0,1:T(8,128)(2,1)S(1)}, u32[]{:S(2)}) copy-start(bf16[64,32]{0,1:T(8,128)(2,1)S(1)} %multiply_convert_fusion.4) | copy-start | bytes 12292
  578.0 18.5 %copy-start.12 = (bf16[8,256,128]{1,2,0:T(8,128)(2,1)S(1)}, bf16[8,256,128]{1,2,0:T(8,128)(2,1)}, u32[]{:S(2)}) copy-start(bf16[8,256,128]{1,2,0:T(8,128)(2,1)} %copy-done.11) | copy-start | bytes 1572868
  578.0 18.7 %copy-start.19 = (f32[8,256,256]{1,2,0:T(8,128)S(1)}, f32[8,256,256]{1,2,0:T(8,128)}, u32[]{:S(2)}) copy-start(f32[8,256,256]{1,2,0:T(8,128)} %get-tuple-element.56) | copy-start | bytes 6291460
  578.0 18.7 %copy-start.46 = (f32[8,256]{1,0:T(8,128)S(1)}, f32[8,256]{1,0:T(8,128)}, u32[]{:S(2)}) copy-start(f32[8,256]{1,0:T(8,128)} %get-tuple-element.55) | copy-start | bytes 24580
  578.0 57.5 %reduce-scatter.16.cloned.1.call-start = ((), (), s32[]{:S(2)}) async-start(), calls=%async_computation.15 | async-start | bytes 1310720 | tf_op jit(solution)/shard_map/reduce_scatter | solution.py:185
  604.0 4.3 copy-start.41
  604.0 4.3 copy-start.50
  604.0 4.5 copy-start.56
  604.2 4.3 copy-start.17
  604.2 4.4 copy-start.26
  608.6 26.9 %copy-start.6 = (bf16[256,2048]{1,0:T(8,128)(2,1)S(1)}, bf16[256,2048]{1,0:T(8,128)(2,1)}, u32[]{:S(2)}) copy-start(bf16[256,2048]{1,0:T(8,128)(2,1)} %param.16) | copy-start | bytes 3145732
  610.6 28.3 %copy-start.16 = (bf16[256,2048]{1,0:T(8,128)(2,1)S(1)}, bf16[256,2048]{1,0:T(8,128)(2,1)}, u32[]{:S(2)}) copy-start(bf16[256,2048]{1,0:T(8,128)(2,1)} %all-gather.13.cloned.1.call-done) | copy-start | bytes 3145732
  610.6 125.8 %all-gather.9.cloned.1.call-start = ((), (), s32[]{:S(2)}) async-start(), calls=%async_computation.11 | async-start | bytes 1310720 | tf_op jit(solution)/shard_map/all_gather | solution.py:150
  611.3 165.1 %all-gather.15.cloned.1.call-start = ((), (), s32[]{:S(2)}) async-start(), calls=%async_computation.16 | async-start | bytes 1310720 | tf_op jit(solution)/shard_map/all_gather | solution.py:197
  638.8 137.7 %reduce-scatter.20.cloned.1.call-start = ((), (), s32[]{:S(2)}) async-start(), calls=%async_computation.18 | async-start | bytes 4718592 | tf_op jit(solution)/shard_map/reduce_scatter | solution.py:199
  643.2 229.6 %reduce-scatter.18.cloned.1.call-start = ((), (), s32[]{:S(2)}) async-start(), calls=%async_computation.17 | async-start | bytes 5898240 | tf_op jit(solution)/shard_map/reduce_scatter | solution.py:202
  668.2 11.8 %copy-start.14 = (bf16[2048,768]{0,1:T(8,128)(2,1)S(1)}, bf16[2048,768]{0,1:T(8,128)(2,1)}, u32[]{:S(2)}) copy-start(bf16[2048,768]{0,1:T(8,128)(2,1)} %get-tuple-element.31) | copy-start | bytes 9437188
  680.0 10.7 %copy-start.37 = (bf16[64,32]{0,1:T(8,128)(2,1)S(1)}, bf16[64,32]{0,1:T(8,128)(2,1)}, u32[]{:S(2)}) copy-start(bf16[64,32]{0,1:T(8,128)(2,1)} %copy-done.36) | copy-start | bytes 12292
  680.0 56.4 %copy-start.39 = (f32[2048]{0:T(1024)S(1)}, f32[2048]{0:T(1024)}, u32[]{:S(2)}) copy-start(f32[2048]{0:T(1024)} %get-tuple-element.18) | copy-start | bytes 24580
  775.8 104.1 %copy-start.1 = (bf16[4,192,2048]{2,1,0:T(8,128)(2,1)S(1)}, bf16[4,192,2048]{2,1,0:T(8,128)(2,1)}, u32[]{:S(2)}) copy-start(bf16[4,192,2048]{2,1,0:T(8,128)(2,1)} %param.31) | copy-start | bytes 9437188
  872.8 6.1 copy-start.24
  (24 other events, 49.6 us)
Sparse Core Ops, SparseCore 0:
  33.6 33.8 reduce-scatter.9
  71.0 77.0 all-gather.6
  151.5 75.6 all-gather.10
  258.9 16.0 reduce-scatter.21
  278.6 148.7 reduce-scatter.13
  429.5 146.1 reduce-scatter.11
  578.1 12.5 all-gather.12
  610.7 24.7 reduce-scatter.15
  637.1 16.6 all-gather.8
  655.8 16.6 all-gather.14
  676.1 90.4 reduce-scatter.19
  770.1 102.6 reduce-scatter.17

commit v2 on v1

--- a/solution.py
+++ b/solution.py
@@ -1,7 +1,13 @@
+import functools
+
 import jax
 import jax.numpy as jnp
 from jax import lax
+from jax.experimental import pallas as pl
+from jax.experimental.pallas import tpu as pltpu
 from jax.sharding import PartitionSpec as P
+
+MESH = pl.DeviceIdType.MESH
 
 HEAD_DIMENSION = 128
 EPSILON = 1e-06
@@ -17,6 +23,160 @@
     return lax.dot_general(a, b, dims, preferred_element_type=F32)
 
 
+def place():
+    e, t = lax.axis_index("exp"), lax.axis_index("tp")
+    return e // 2, e % 2, t // 2, t % 2
+
+def dev(z, y, x, c):
+    return (z * 2 + y, x * 2 + c)
+
+def geometry():
+    z, y, x, c = place()
+    first = c == 0
+    a, b = jnp.where(first, x, y), jnp.where(first, y, x)
+    nbr_a = dev(z, jnp.where(first, y, 1 - y), jnp.where(first, 1 - x, x), c)
+    nbr_b = dev(z, jnp.where(first, 1 - y, y), jnp.where(first, x, 1 - x), c)
+    low = z < 2
+    m = jnp.where(low, z, 3 - z)
+    step = jnp.where(low, 1, -1)
+    mir = lambda k: jnp.where(low, k, 3 - k)
+    ahead = dev(z + step, y, x, c)
+    back = dev(jnp.where(m == 0, z, z - step), y, x, c)
+    return z, y, x, c, a, b, nbr_a, nbr_b, m, mir, ahead, back, dev(z, y, x, 1 - c)
+
+def greet(ids, extra, extra_ok):
+    barrier = pltpu.get_barrier_semaphore()
+    for d in ids:
+        pl.semaphore_signal(barrier, inc=1, device_id=d, device_id_type=MESH)
+    @pl.when(extra_ok)
+    def _():
+        pl.semaphore_signal(barrier, inc=1, device_id=extra, device_id_type=MESH)
+    pl.semaphore_wait(barrier, len(ids) + jnp.where(extra_ok, 1, 0))
+
+def rcopy(src, dst, ss, rs, d):
+    return pltpu.make_async_remote_copy(src_ref=src, dst_ref=dst, send_sem=ss, recv_sem=rs, device_id=d, device_id_type=MESH)
+
+def rows_loop(n, step, fn):
+    def it(i, _):
+        fn(pl.ds(pl.multiple_of(i * step, step), step))
+        return 0
+    lax.fori_loop(0, n // step, it, 0)
+
+def rs_kernel(part, out, own, prt, ra, r, rb, s_own, s_cs, s_cr, s_as, s_ar, s_zs, s_zr, s_bs, s_br):
+    z, y, x, c, a, b, nbr_a, nbr_b, m, mir, ahead, back, mate = geometry()
+    q = out.shape[0]
+    block = 4 * q
+    greet([mate, nbr_a, nbr_b, ahead], back, m == 1)
+    order = [mir(3), mir(2), mir(jnp.where(m == 0, 1, 0)), z]
+
+    def src(k, i, j, core):
+        yy = jnp.where(core == 0, j, i)
+        xx = jnp.where(core == 0, i, j)
+        return part.at[pl.ds(pl.multiple_of((k * 2 + yy) * block + (xx * 2 + core) * q, q), q)]
+
+    for n, k in enumerate(order):
+        for i in range(2):
+            for j in range(2):
+                rcopy(src(k, i, j, 1 - c), prt.at[k, i, j], s_cs.at[n, i, j], s_cr.at[n, i, j], mate).start()
+        for i in range(2):
+            for j in range(2):
+                pltpu.make_async_copy(src(k, i, j, c), own.at[k, i, j], s_own.at[n, i, j]).start()
+    for n, k in enumerate(order):
+        for i in range(2):
+            for j in range(2):
+                pltpu.make_async_copy(src(k, i, j, c), own.at[k, i, j], s_own.at[n, i, j]).wait()
+                rcopy(src(k, i, j, 1 - c), prt.at[k, i, j], s_cs.at[n, i, j], s_cr.at[n, i, j], mate).wait()
+        for j in range(2):
+            def add(rows, j=j, k=k):
+                own[k, 1 - a, j, rows, :] = (own[k, 1 - a, j, rows, :].astype(F32) + prt[k, 1 - a, j, rows, :].astype(F32)).astype(BF)
+            rows_loop(q, 16, add)
+        rcopy(own.at[k, 1 - a], ra.at[k], s_as.at[n], s_ar.at[n], nbr_a).start()
+    for n, k in enumerate(order[:3]):
+        rcopy(own.at[k, 1 - a], ra.at[k], s_as.at[n], s_ar.at[n], nbr_a).wait()
+        slot_in = n
+        def wait_r(k=k, n=n):
+            rcopy(own.at[k, a], r.at[n], s_zs.at[n], s_zr.at[n], ahead).wait_recv()
+        @pl.when(m == 1)
+        def _(k=k, n=n):
+            wait_r(k, n)
+            for j in range(2):
+                def add(rows, j=j):
+                    own[k, a, j, rows, :] = (own[k, a, j, rows, :].astype(F32) + prt[k, a, j, rows, :].astype(F32)
+                        + ra[k, j, rows, :].astype(F32) + r[n, j, rows, :].astype(F32)).astype(BF)
+                rows_loop(q, 16, add)
+        @pl.when(m == 0)
+        def _(k=k, n=n):
+            for j in range(2):
+                def add(rows, j=j):
+                    own[k, a, j, rows, :] = (own[k, a, j, rows, :].astype(F32) + prt[k, a, j, rows, :].astype(F32)
+                        + ra[k, j, rows, :].astype(F32)).astype(BF)
+                rows_loop(q, 16, add)
+        if n < 2:
+            slot = jnp.where(m == 0, n, n + 2)
+            rcopy(own.at[k, a], r.at[slot], s_zs.at[n], s_zr.at[slot], ahead).start()
+        else:
+            @pl.when(m == 0)
+            def _(k=k, n=n):
+                rcopy(own.at[k, a], r.at[4], s_zs.at[n], s_zr.at[4], ahead).start()
+            @pl.when(m == 1)
+            def _(k=k, n=n):
+                rcopy(own.at[k, a], r.at[3], s_zs.at[n], s_zr.at[3], back).start()
+    k, n = z, 3
+    rcopy(own.at[k, 1 - a], ra.at[k], s_as.at[n], s_ar.at[n], nbr_a).wait()
+    rcopy(own.at[k, a], r.at[3], s_zs.at[0], s_zr.at[3], ahead).wait_recv()
+
+    def total(j, rows):
+        return (own[k, a, j, rows, :].astype(F32) + prt[k, a, j, rows, :].astype(F32)
+            + ra[k, j, rows, :].astype(F32) + r[3, j, rows, :].astype(F32))
+    @pl.when(m == 1)
+    def _():
+        rcopy(own.at[k, a], r.at[4], s_zs.at[0], s_zr.at[4], ahead).wait_recv()
+        def add(rows):
+            own[k, a, 1 - b, rows, :] = (total(1 - b, rows) + r[4, 1 - b, rows, :].astype(F32)).astype(BF)
+        rows_loop(q, 16, add)
+    @pl.when(m == 0)
+    def _():
+        def add(rows):
+            own[k, a, 1 - b, rows, :] = total(1 - b, rows).astype(BF)
+        rows_loop(q, 16, add)
+    last = rcopy(own.at[k, a, 1 - b], rb, s_bs, s_br, nbr_b)
+    last.start()
+    @pl.when(m == 1)
+    def _():
+        def add(rows):
+            out[rows, :] = total(b, rows) + r[4, b, rows, :].astype(F32)
+        rows_loop(q, 16, add)
+    @pl.when(m == 0)
+    def _():
+        def add(rows):
+            out[rows, :] = total(b, rows)
+        rows_loop(q, 16, add)
+    last.wait()
+    def add(rows):
+        out[rows, :] = out[rows, :] + rb[rows, :].astype(F32)
+    rows_loop(q, 16, add)
+    for n, k in enumerate(order[:3]):
+        rcopy(own.at[k, a], r.at[0], s_zs.at[n], s_zr.at[0], ahead).wait_send()
+
+def reduce_scatter(part, cid):
+    rows, width = part.shape
+    q = rows // 32
+    dma = lambda *s: pltpu.SemaphoreType.DMA(s)
+    return pl.pallas_call(
+        rs_kernel,
+        out_shape=jax.ShapeDtypeStruct((q, width), F32),
+        in_specs=[pl.BlockSpec(memory_space=pl.ANY)],
+        out_specs=pl.BlockSpec(memory_space=pltpu.VMEM),
+        scratch_shapes=[
+            pltpu.VMEM((4, 2, 2, q, width), BF), pltpu.VMEM((4, 2, 2, q, width), BF),
+            pltpu.VMEM((4, 2, q, width), BF), pltpu.VMEM((5, 2, q, width), BF), pltpu.VMEM((q, width), BF),
+            dma(4, 2, 2), dma(4, 2, 2), dma(4, 2, 2), dma(4), dma(4), dma(3), dma(5),
+            pltpu.SemaphoreType.DMA, pltpu.SemaphoreType.DMA,
+        ],
+        compiler_params=pltpu.CompilerParams(collective_id=cid, has_side_effects=True),
+    )(part)
+
+
 def rotate_normed(pre_proj, gain_vec, cosine, sine):
     normed = (
         pre_proj * lax.rsqrt(jnp.mean(pre_proj * pre_proj, -1, keepdims=True) + EPSILON) * gain_vec
@@ -30,6 +190,7 @@
 
 
 def body(
+    near,
     tokens,
     cotangent,
     seq_start,
@@ -145,8 +306,12 @@
     ).astype(BF)
     glog_all = gather_all(grad_logits)
 
-    dx = lax.psum_scatter(dx_part, both, scatter_dimension=0, tiled=True).astype(F32)
-    mixture = lax.psum_scatter(mix_part, both, scatter_dimension=0, tiled=True).astype(F32)
+    if near:
+        dx = reduce_scatter(dx_part, 1)
+        mixture = reduce_scatter(mix_part, 1)
+    else:
+        dx = lax.psum_scatter(dx_part, both, scatter_dimension=0, tiled=True).astype(F32)
+        mixture = lax.psum_scatter(mix_part, both, scatter_dimension=0, tiled=True).astype(F32)
     layer_out = lax.all_gather((after + mixture).astype(BF), "tp", axis=0, tiled=True)
 
     grad_n2 = dx + dot(grad_logits, w_router, LAST)
@@ -227,10 +392,23 @@
     )
 
 
+def is_near(mesh):
+    devices = mesh.devices
+    if devices.shape != (8, 4):
+        return False
+    low = devices[0, 0].coords
+    return all(
+        tuple(p - o for p, o in zip(devices[e, t].coords, low)) + (devices[e, t].core_on_chip,)
+        == (t // 2, e % 2, e // 2, t % 2)
+        for e in range(8)
+        for t in range(4)
+    )
+
+
 def solution(mesh):
     e, t = "exp", "tp"
     return jax.shard_map(
-        body,
+        functools.partial(body, is_near(mesh)),
         mesh=mesh,
         in_specs=(
             P(e, None), P(e, None), P(e), P(e, None), P(), P(), P(), P(),

time: 893 us -> 723 us (0.81)
  waiting for transfers between devices: 545 us -> 267 us
  Pallas kernels: 0 us -> 114 us
  blocking collectives: 124 us -> 114 us
    reduce_scatter x2 -> x0, waiting for transfers between devices: 282 us -> none  [the longest x1 146 us: body(): lax.psum_scatter(mix_part, both, scatter_dimension=0, tiled=True)]
    pallas_call x0 -> x2, Pallas kernels: none -> 114 us  [reduce_scatter(): pl.pallas_call(rs_kernel, out_shape=jax.ShapeDtypeStruct((q, width), F32)...]
    all_to_all x1 -> x0, blocking collectives: 10.6 us -> none  [body(): lax.all_to_all(gates_part, 'exp', split_axis=0, concat_axis=1, tiled=True)]
  transfers between devices with their start and end apart: 12 -> 11, of which waited for: 8 -> 6; matrix products, arithmetic and copies ran while one was open for 13% -> 16% of each run, Pallas kernels for 0% -> 16%
where the time goes in v2:
time: 723 us; the launch traced here: 716 us
  waiting for transfers between devices  267 us (37%)
  matrix products  140 us (19%)
  blocking collectives  114 us (16%)
  Pallas kernels  114 us (16%)
  local copies, waits for them, and re-layouts  31.8 us (4%)
  other arithmetic  29.6 us (4%)
  between operations  15.5 us (2%)
    dot_general x19, matrix products, dot(): return lax.dot_general(a, b, dims, preferred_element_type=F32)  131 us
    pallas_call x2, Pallas kernels, reduce_scatter(): pl.pallas_call(rs_kernel, out_shape=jax.ShapeDtypeStruct((q, width), F32)...  114 us
    all_gather x2, waiting for transfers between devices, gather_all(): return lax.all_gather(a, both, axis=0, tiled=True)  98.7 us
    reduce_scatter x1, waiting for transfers between devices, body(): lax.psum_scatter(qkv_part.astype(BF), 'exp', scatter_dimension=0, tiled=T...  94 us
    all_gather x1, blocking collectives, gather_all(): return lax.all_gather(a, both, axis=0, tiled=True)  43.2 us
    psum x1, blocking collectives, body(): small = lax.psum(small, both)  39.1 us
    reduce_scatter x1, waiting for transfers between devices, body(): lax.psum_scatter(attn_part, 'tp', scatter_dimension=0, tiled=True)  34 us
    all_gather x1, blocking collectives, body(): routes_all = lax.all_gather(routes, 'exp', axis=0, tiled=True)  31.4 us
  transfers between devices with their start and end apart: 11, of which 6 were waited for; matrix products, arithmetic and copies ran while one was open for 16% of the time, Pallas kernels for 16%

profile of v2, /device:TPU:0, one launch (start us, length us, event | category | flops | bytes accessed | tf_op | source)
XLA Modules:
  0.0 716.3 jit_solution(16047862173620695834)
XLA Ops:
  7.3 1.6 fusion.48
  9.5 1.5 fusion.7
  11.1 2.0 multiply_reduce_fusion.4
  15.3 3.9 convolution_bitcast_fusion
  21.1 1.4 fusion.45
  22.6 4.1 fusion.98
  26.7 1.9 fusion.31
  30.8 2.6 fusion.100
  33.5 34.0 %reduce-scatter.8.cloned.1.call-done = f32[64,2048]{1,0:T(8,128)} async-done(((f32[256,2048]{1,0:T(8,128)}), f32[64,2048]{1,0:T(8,128)}) %reduce-scatter.8.cloned.1.call-update) | async-done | bytes 524304 | tf_op jit(solution)/shard_map/reduce_scatter | solution.py:272
  67.5 1.3 multiply_reduce_fusion.3
  70.5 1.7 constant_dynamic-slice_fusion
  72.2 31.4 %all_gather.21 = s32[2048,8]{0,1:T(8,128)S(1)} all-gather(s32[256,8]{0,1:T(8,128)S(1)} %copy-done.48), channel_id=1, replica_groups=mesh['exp'=8,'tp'=4] {'exp'}, dimensions={0}, use_global_device_ids=true | all-gather | bytes 73728 | tf_op jit(solution)/shard_map/all_gather | solution.py:230
  103.9 44.2 %all-gather.7.cloned.1.call-done = bf16[2048,2048]{1,0:T(8,128)(2,1)} async-done(((bf16[64,2048]{1,0:T(8,128)(2,1)}), bf16[2048,2048]{1,0:T(8,128)(2,1)}) %all-gather.7.cloned.1.call-update) | async-done | bytes 8388624 | tf_op jit(solution)/shard_map/all_gather | solution.py:227
  148.0 6.1 fusion.99
  155.1 17.6 %fusion.4 = f32[2048,1536]{0,1:T(8,128)} fusion(bf16[2048,2048]{1,0:T(8,128)(2,1)S(1)} %copy-done.2, bf16[2048,768]{0,1:T(8,128)(2,1)S(1)} %bitcast.216, bf16[2048,768]{0,1:T(8,128)(2,1)} %bitcast.217), kind=kOutput, calls=%fused_computation.15 | convolution fusion | flops 12897484800 | bytes 27262976 | tf_op jit(solution)/shard_map/dot_general | solution.py:23
  172.6 54.5 %all-gather.11.cloned.1.call-done = bf16[2048,2048]{1,0:T(8,128)(2,1)} async-done(((bf16[64,2048]{1,0:T(8,128)(2,1)}), bf16[2048,2048]{1,0:T(8,128)(2,1)}) %all-gather.11.cloned.1.call-update) | async-done | bytes 8388624 | tf_op jit(solution)/shard_map/all_gather | solution.py:227
  227.2 17.0 %multiply_convert_fusion.1 = (bf16[2048,768]{0,1:T(8,128)(2,1)}, bf16[2048,768]{0,1:T(8,128)(2,1)}, f32[2048,768]{0,1:T(8,128)}, bf16[2048,768]{0,1:T(8,128)(2,1)}) fusion(f32[2048,1536]{0,1:T(8,128)} %fusion.4, f32[2048,4]{0,1:T(4,128)S(1)} %constant_dynamic-slice_fusion.1, bf16[2048,2048]{1,0:T(8,128)(2,1)} %all-gather.11.cloned.1.call-done, ...), kind=kOutput, calls=%fused_computation.10 | convolution fusion | flops 6470762496 | bytes 39878656 | tf_op jit(solution)/shard_map/dot_general | solution.py:23
  244.1 3.8 reduce_sum.175
  247.9 4.1 all-to-all-start
  252.3 19.4 %convolution_convert_fusion.1.part = bf16[2048,2048]{1,0:T(8,128)(2,1)} fusion(bf16[2048,768]{0,1:T(8,128)(2,1)} %get-tuple-element.29, bf16[2048,768]{0,1:T(8,128)(2,1)} %get-tuple-element.28, bf16[2048,768]{0,1:T(8,128)(2,1)} %bitcast.215, bf16[2048,768]{0,1:T(8,128)(2,1)} %bitcast.218), kind=kOutput, calls=%fused_computation.4 | convolution fusion | flops 12914262016 | bytes 20971520 | tf_op jit(solution)/shard_map/dot_general | solution.py:23
  272.6 11.0 %convolution_convert_fusion.2.part = bf16[2048,2048]{1,0:T(8,128)(2,1)} fusion(bf16[2048,768]{0,1:T(8,128)(2,1)} %get-tuple-element.31, bf16[768,2048]{1,0:T(8,128)(2,1)S(1)} %bitcast.202), kind=kOutput, calls=%fused_computation.5 | convolution fusion | flops 6446645248 | bytes 14680064 | tf_op jit(solution)/shard_map/dot_general | solution.py:23
  283.6 56.4 %shard_map.264 = f32[64,2048]{1,0:T(8,128)} custom-call(bf16[2048,2048]{1,0:T(8,128)(2,1)} %convolution_convert_fusion.1.part), custom_call_target="tpu_custom_call" | custom-call | tf_op jit(solution)/shard_map/pallas_call | solution.py:165
  340.1 57.6 %shard_map.263 = f32[64,2048]{1,0:T(8,128)} custom-call(bf16[2048,2048]{1,0:T(8,128)(2,1)} %convolution_convert_fusion.2.part), custom_call_target="tpu_custom_call" | custom-call | tf_op jit(solution)/shard_map/pallas_call | solution.py:165
  401.2 2.4 fusion.93
  403.7 15.5 %all-gather.13.cloned.1.call-done = bf16[256,2048]{1,0:T(8,128)(2,1)} async-done(((bf16[64,2048]{1,0:T(8,128)(2,1)}), bf16[256,2048]{1,0:T(8,128)(2,1)}) %all-gather.13.cloned.1.call-update) | async-done | bytes 1048592 | tf_op jit(solution)/shard_map/all_gather | solution.py:325
  419.2 4.6 convolution_convert_fusion.5
  423.8 1.2 copy.82
  425.2 1.3 multiply_convert_fusion.2
  427.1 1.3 fusion.14
  428.5 1.5 fusion.15
  432.7 3.7 fusion.101
  437.6 1.4 fusion.5
  440.0 24.1 %reduce-scatter.10.cloned.1.call-done = bf16[64,2048]{1,0:T(8,128)(2,1)} async-done(((bf16[256,2048]{1,0:T(8,128)(2,1)}), bf16[64,2048]{1,0:T(8,128)(2,1)}) %reduce-scatter.10.cloned.1.call-update) | async-done | bytes 262160 | tf_op jit(solution)/shard_map/reduce_scatter | solution.py:350
  465.2 2.0 fusion.40
  467.4 4.3 convolution_convert_fusion.3
  472.7 4.0 convolution_convert_fusion
  476.8 1.9 copy-done.15
  478.6 18.1 %fusion.3 = f32[2048,1536]{0,1:T(8,128)} fusion(bf16[2048,2048]{1,0:T(8,128)(2,1)} %all-gather.7.cloned.1.call-done, bf16[2048,768]{0,1:T(8,128)(2,1)} %get-tuple-element.29, bf16[2048,768]{0,1:T(8,128)(2,1)S(1)} %copy-done.15), kind=kOutput, calls=%fused_computation.14 | convolution fusion | flops 12897484800 | bytes 27262976 | tf_op jit(solution)/shard_map/dot_general | solution.py:23
  496.7 11.8 %fusion.94 = (f32[2048,768]{0,1:T(8,128)}, f32[2048,768]{0,1:T(8,128)}) fusion(f32[2048,1536]{0,1:T(8,128)} %fusion.3), kind=kLoop, calls=%fused_computation.171 | loop fusion | bytes 25165824 | tf_op jit(solution)/shard_map/slice | solution.py:390
  508.5 10.7 %fusion.102 = f32[768,2048]{1,0:T(8,128)} fusion(bf16[2048,768]{0,1:T(8,128)(2,1)S(1)} %copy-done.14, bf16[2048,2048]{1,0:T(8,128)(2,1)} %all-gather.11.cloned.1.call-done), kind=kOutput, calls=%fused_computation.179 | convolution fusion | flops 6442450944 | bytes 17825792 | tf_op jit(solution)/shard_map/dot_general | solution.py:23
  519.2 43.2 %all-gather = bf16[32,64,32]{1,2,0:T(8,128)(2,1)S(1)} all-gather(bf16[1,64,32]{1,2,0:T(8,128)(2,1)S(1)} %bitcast.214), channel_id=1, replica_groups=mesh['exp'=8,'tp'=4] {'exp','tp'}, dimensions={0}, use_global_device_ids=true | all-gather | bytes 135168 | tf_op jit(solution)/shard_map/all_gather | solution.py:227
  562.8 2.1 fusion.26
  564.9 39.1 %psum.7 = f32[4352]{0:T(1024)S(1)} all-reduce(f32[4352]{0:T(1024)S(1)} %pad_maximum_fusion.7), channel_id=1, replica_groups=mesh['exp'=8,'tp'=4] {'exp','tp'}, use_global_device_ids=true, to_apply=%region_23.24 | all-reduce | flops 4352 | bytes 34816 | tf_op jit(solution)/shard_map/psum | solution.py:372
  605.1 2.9 convert_element_type.163
  608.0 94.0 %reduce-scatter.12.cloned.1.call-done = bf16[256,1280]{1,0:T(8,128)(2,1)} async-done(((bf16[2048,1280]{1,0:T(8,128)(2,1)}), bf16[256,1280]{1,0:T(8,128)(2,1)}) %reduce-scatter.12.cloned.1.call-update) | async-done | bytes 655376 | tf_op jit(solution)/shard_map/reduce_scatter | solution.py:367
  702.0 2.2 slice.70
  704.2 1.6 fusion.95
  705.8 2.3 copy.116
  (192 shorter events, 24.5 us)
Async XLA Ops:
  7.2 220.0 %copy-start = (bf16[4,192,2048]{2,1,0:T(8,128)(2,1)S(1)}, bf16[4,192,2048]{2,1,0:T(8,128)(2,1)}, u32[]{:S(2)}) copy-start(bf16[4,192,2048]{2,1,0:T(8,128)(2,1)} %param.31) | copy-start | bytes 9437188
  7.2 60.3 %reduce-scatter.8.cloned.1.call-start = ((), (), s32[]{:S(2)}) async-start(), calls=%async_computation.6 | async-start | bytes 2621440 | tf_op jit(solution)/shard_map/reduce_scatter | solution.py:272
  7.3 7.7 %copy-start.50 = (f32[64]{0:T(128)}, f32[64]{0:T(128)S(1)}, u32[]{:S(2)}) copy-start(f32[64]{0:T(128)S(1)} %negate_power_fusion) | copy-start | bytes 772
  9.5 5.4 copy-start.43
  11.1 8.6 %copy-start.45 = (f32[256]{0:T(256)}, f32[256]{0:T(256)S(1)}, u32[]{:S(2)}) copy-start(f32[256]{0:T(256)S(1)} %add_rsqrt_fusion) | copy-start | bytes 3076
  14.2 7.0 copy-start.23
  15.3 5.0 copy-start.5
  15.3 5.0 copy-start.28
  15.3 4.9 copy-start.32
  15.3 5.4 copy-start.54
  20.8 7.9 %copy-start.39 = (bf16[256,128,1]{1,0,2:T(8,128)(2,1)}, bf16[256,128,1]{1,0,2:T(8,128)(2,1)S(1)}, u32[]{:S(2)}) copy-start(bf16[256,128,1]{1,0,2:T(8,128)(2,1)S(1)} %fusion.16) | copy-start | bytes 196612
  26.7 4.1 copy-start.59
  30.8 38.8 %copy-start.33 = (f32[2048]{0:T(1024)S(1)}, f32[2048]{0:T(1024)}, u32[]{:S(2)}) copy-start(f32[2048]{0:T(1024)} %param.21) | copy-start | bytes 24580
  33.4 38.8 %copy-start.48 = (s32[256,8]{0,1:T(8,128)S(1)}, s32[256,8]{0,1:T(8,128)}, u32[]{:S(2)}) copy-start(s32[256,8]{0,1:T(8,128)} %param.19) | copy-start | bytes 24580
  33.4 114.6 %all-gather.7.cloned.1.call-start = ((), (), s32[]{:S(2)}) async-start(), calls=%async_computation.7 | async-start | bytes 8650752 | tf_op jit(solution)/shard_map/all_gather | solution.py:227
  70.4 156.7 %all-gather.11.cloned.1.call-start = ((), (), s32[]{:S(2)}) async-start(), calls=%async_computation.9 | async-start | bytes 8650752 | tf_op jit(solution)/shard_map/all_gather | solution.py:227
  148.0 7.0 copy-start.2
  148.0 7.0 copy-start.60
  247.9 23.8 %all-to-all-start = ((f32[8,256,4]{1,2,0:T(4,128)}), f32[8,256,4]{1,2,0:T(4,128)S(1)}, u32[]{:S(2)}, u32[]{:S(2)}) async-start(f32[8,256,4]{1,2,0:T(4,128)} %bitcast.18), calls=%async_computation.1 | async-start | bytes 65536 | tf_op jit(solution)/shard_map/all_to_all | solution.py:301
  252.1 145.7 %reduce-scatter.16.cloned.1.call-start = ((), (), s32[]{:S(2)}) async-start(), calls=%async_computation.15 | async-start | bytes 163840
  272.5 146.7 %all-gather.13.cloned.1.call-start = ((), (), s32[]{:S(2)}) async-start(), calls=%async_computation.10 | async-start | bytes 1310720 | tf_op jit(solution)/shard_map/all_gather | solution.py:325
  340.0 60.1 %copy-start.10 = (f32[64,2048]{1,0:T(8,128)S(1)}, f32[64,2048]{1,0:T(8,128)}, u32[]{:S(2)}) copy-start(f32[64,2048]{1,0:T(8,128)} %copy-done.9) | copy-start | bytes 1572868
  340.0 60.1 %copy-start.17 = (f32[64,2048]{1,0:T(8,128)S(1)}, f32[64,2048]{1,0:T(8,128)}, u32[]{:S(2)}) copy-start(f32[64,2048]{1,0:T(8,128)} %shard_map.264) | copy-start | bytes 1572868
  340.0 60.1 %copy-start.26 = (bf16[2048,32]{0,1:T(8,128)(2,1)S(1)}, bf16[2048,32]{0,1:T(8,128)(2,1)}, u32[]{:S(2)}) copy-start(bf16[2048,32]{0,1:T(8,128)(2,1)} %param.28) | copy-start | bytes 393220
  340.1 60.1 %copy-start.34 = (f32[2048]{0:T(1024)S(1)}, f32[2048]{0:T(1024)}, u32[]{:S(2)}) copy-start(f32[2048]{0:T(1024)} %param.21) | copy-start | bytes 24580
  340.1 60.1 %copy-start.53 = (f32[64]{0:T(128)S(1)}, f32[64]{0:T(128)}, u32[]{:S(2)}) copy-start(f32[64]{0:T(128)} %copy-done.52) | copy-start | bytes 772
  340.1 61.2 %copy-start.58 = (f32[64]{0:T(128)S(1)}, f32[64]{0:T(128)}, u32[]{:S(2)}) copy-start(f32[64]{0:T(128)} %get-tuple-element.51) | copy-start | bytes 772
  400.2 23.6 %copy-start.37 = (bf16[64,32]{0,1:T(8,128)(2,1)}, bf16[64,32]{0,1:T(8,128)(2,1)S(1)}, u32[]{:S(2)}) copy-start(bf16[64,32]{0,1:T(8,128)(2,1)S(1)} %multiply_convert_fusion.4) | copy-start | bytes 12292
  403.6 21.4 %copy-start.12 = (bf16[8,256,128]{1,2,0:T(8,128)(2,1)S(1)}, bf16[8,256,128]{1,2,0:T(8,128)(2,1)}, u32[]{:S(2)}) copy-start(bf16[8,256,128]{1,2,0:T(8,128)(2,1)} %copy-done.11) | copy-start | bytes 1572868
  403.7 21.5 %copy-start.20 = (f32[8,256,256]{1,2,0:T(8,128)S(1)}, f32[8,256,256]{1,2,0:T(8,128)}, u32[]{:S(2)}) copy-start(f32[8,256,256]{1,2,0:T(8,128)} %get-tuple-element.56) | copy-start | bytes 6291460
  403.7 21.5 %copy-start.47 = (f32[8,256]{1,0:T(8,128)S(1)}, f32[8,256]{1,0:T(8,128)}, u32[]{:S(2)}) copy-start(f32[8,256]{1,0:T(8,128)} %get-tuple-element.55) | copy-start | bytes 24580
  403.7 60.3 %reduce-scatter.10.cloned.1.call-start = ((), (), s32[]{:S(2)}) async-start(), calls=%async_computation.11 | async-start | bytes 1310720 | tf_op jit(solution)/shard_map/reduce_scatter | solution.py:350
  432.5 4.3 copy-start.42
  432.5 4.3 copy-start.49
  432.5 4.5 copy-start.57
  432.7 4.3 copy-start.18
  432.7 4.4 copy-start.27
  437.1 26.9 %copy-start.6 = (bf16[256,2048]{1,0:T(8,128)(2,1)S(1)}, bf16[256,2048]{1,0:T(8,128)(2,1)}, u32[]{:S(2)}) copy-start(bf16[256,2048]{1,0:T(8,128)(2,1)} %param.16) | copy-start | bytes 3145732
  439.0 28.3 %copy-start.16 = (bf16[256,2048]{1,0:T(8,128)(2,1)S(1)}, bf16[256,2048]{1,0:T(8,128)(2,1)}, u32[]{:S(2)}) copy-start(bf16[256,2048]{1,0:T(8,128)(2,1)} %all-gather.13.cloned.1.call-done) | copy-start | bytes 3145732
  439.1 125.9 %all-gather.9.cloned.1.call-start = ((), (), s32[]{:S(2)}) async-start(), calls=%async_computation.8 | async-start | bytes 1310720 | tf_op jit(solution)/shard_map/all_gather | solution.py:315
  439.8 165.3 %all-gather.15.cloned.1.call-start = ((), (), s32[]{:S(2)}) async-start(), calls=%async_computation.12 | async-start | bytes 1310720 | tf_op jit(solution)/shard_map/all_gather | solution.py:362
  467.3 137.8 %reduce-scatter.14.cloned.1.call-start = ((), (), s32[]{:S(2)}) async-start(), calls=%async_computation.14 | async-start | bytes 4718592 | tf_op jit(solution)/shard_map/reduce_scatter | solution.py:364
  471.7 230.3 %reduce-scatter.12.cloned.1.call-start = ((), (), s32[]{:S(2)}) async-start(), calls=%async_computation.13 | async-start | bytes 5898240 | tf_op jit(solution)/shard_map/reduce_scatter | solution.py:367
  496.7 11.8 %copy-start.14 = (bf16[2048,768]{0,1:T(8,128)(2,1)S(1)}, bf16[2048,768]{0,1:T(8,128)(2,1)}, u32[]{:S(2)}) copy-start(bf16[2048,768]{0,1:T(8,128)(2,1)} %get-tuple-element.31) | copy-start | bytes 9437188
  508.5 10.7 %copy-start.38 = (bf16[64,32]{0,1:T(8,128)(2,1)S(1)}, bf16[64,32]{0,1:T(8,128)(2,1)}, u32[]{:S(2)}) copy-start(bf16[64,32]{0,1:T(8,128)(2,1)} %copy-done.37) | copy-start | bytes 12292
  508.5 56.4 %copy-start.40 = (f32[2048]{0:T(1024)S(1)}, f32[2048]{0:T(1024)}, u32[]{:S(2)}) copy-start(f32[2048]{0:T(1024)} %get-tuple-element.18) | copy-start | bytes 24580
  604.5 104.5 %copy-start.1 = (bf16[4,192,2048]{2,1,0:T(8,128)(2,1)S(1)}, bf16[4,192,2048]{2,1,0:T(8,128)(2,1)}, u32[]{:S(2)}) copy-start(bf16[4,192,2048]{2,1,0:T(8,128)(2,1)} %param.31) | copy-start | bytes 9437188
  702.0 6.1 copy-start.25
  (24 other events, 49.5 us)
Sparse Core Ops, SparseCore 0:
  33.6 33.8 reduce-scatter.7
  70.9 77.0 all-gather.6
  151.4 75.6 all-gather.10
  272.6 20.1 reduce-scatter.15
  403.8 15.3 all-gather.12
  439.2 24.7 reduce-scatter.9
  465.6 16.6 all-gather.8
  484.4 16.6 all-gather.14
  504.8 90.9 reduce-scatter.13
  599.2 102.6 reduce-scatter.11
